TPU v7x, 32 devices: a 4x2x2 block of a 4x4x8 slice. The times are simulated.
32 devices in a mesh: dp: 4 (over y, z), cp: 8 (over x, core).
Axes of the slice: x: 4, y: 2, z: 2, core: 2. Of those that a mesh axis runs over, the one named last changes fastest.
The devices are a block of a 4x4x8 slice.
Arguments:
- q_raw: bfloat16 [16384, 32, 128], P(('dp', 'cp')), parts along dimension 0
- k_raw: bfloat16 [16384, 8, 128], P(('dp', 'cp')), parts along dimension 0
- v_proj: bfloat16 [16384, 8, 128], P(('dp', 'cp')), parts along dimension 0
- out_fwd: bfloat16 [16384, 32, 128], P(('dp', 'cp')), parts along dimension 0
- lse_fwd: float32 [16384, 32], P(('dp', 'cp')), parts along dimension 0
- d_out: bfloat16 [16384, 32, 128], P(('dp', 'cp')), parts along dimension 0
- q_norm: float32 [128], replicated
- k_norm: float32 [128], replicated
Outputs:
- output 1: bfloat16 [16384, 32, 128], P(('dp', 'cp')), parts along dimension 0
- output 2: bfloat16 [16384, 8, 128], P(('dp', 'cp')), parts along dimension 0
- output 3: bfloat16 [16384, 8, 128], P(('dp', 'cp')), parts along dimension 0
- output 4: float32 [512], P('dp'), parts along dimension 0
- output 5: float32 [512], P('dp'), parts along dimension 0
There are 4 independent parts. A program takes and returns all parts, laid end to end along the dimension named above; an argument that names none is the same for every part.
All inputs are finite; a program needn't handle non-finite values.
Results may differ from a plain program's by a relative error of at most 0.00271093.
Values are sent between devices in bfloat16 or wider.
A program may use at most 768 MiB of HBM per device.

v0:
```python
import jax
import jax.numpy as jnp
from jax import lax
from jax.sharding import PartitionSpec as P

HEAD_DIM = 128
ROPE_THETA = 1000000.0
NORM_EPS = 1e-6


def rope_tables(positions):
    inv_freq = ROPE_THETA ** (-jnp.arange(0, HEAD_DIM, 2).astype(jnp.float32) / HEAD_DIM)
    angles = positions.astype(jnp.float32)[:, None] * inv_freq[None, :]
    angles = jnp.concatenate([angles, angles], axis=-1)
    return jnp.cos(angles)[:, None, :], jnp.sin(angles)[:, None, :]


def norm_rope(raw_in, weight, cos_t, sin_t):
    mean_sq = jnp.mean(raw_in * raw_in, axis=-1, keepdims=True)
    normed = raw_in * lax.rsqrt(mean_sq + NORM_EPS) * weight
    half_dim = raw_in.shape[-1] // 2
    rotated = jnp.concatenate([-normed[..., half_dim:], normed[..., :half_dim]], axis=-1)
    return normed * cos_t + rotated * sin_t


def pair_grads(q_blk, do_blk, lse_blk, delta_blk, k_blk, v_blk, visible):
    sm_scale = HEAD_DIM ** -0.5
    logits = jnp.einsum('qngd,knd->qngk', q_blk, k_blk, preferred_element_type=jnp.float32) * sm_scale - lse_blk[..., None]
    if visible is not None:
        logits = jnp.where(visible[:, None, None, :], logits, -jnp.inf)
    attn_prob = jnp.exp(logits)
    attn_dprob = jnp.einsum('qngd,knd->qngk', do_blk, v_blk, preferred_element_type=jnp.float32)
    score_grad = (attn_prob * (attn_dprob - delta_blk[..., None])).astype(jnp.bfloat16)
    prob_bf = attn_prob.astype(jnp.bfloat16)
    dq_part = sm_scale * jnp.einsum('qngk,knd->qngd', score_grad, k_blk, preferred_element_type=jnp.float32)
    dk_part = sm_scale * jnp.einsum('qngk,qngd->knd', score_grad, q_blk, preferred_element_type=jnp.float32)
    dv_part = jnp.einsum('qngk,qngd->knd', prob_bf, do_blk, preferred_element_type=jnp.float32)
    return dq_part, dk_part, dv_part


def own_grads(q_b, do_b, lse_b, delta_sum, k_blk, v_blk):
    chunk_len = k_blk.shape[0] // 2
    tri_mask = jnp.arange(chunk_len)[:, None] >= jnp.arange(chunk_len)[None, :]
    dq_first, dk_first, dv_first = pair_grads(q_b[:chunk_len], do_b[:chunk_len], lse_b[:chunk_len], delta_sum[:chunk_len], k_blk[:chunk_len], v_blk[:chunk_len], tri_mask)
    dq_cross, dk_cross, dv_cross = pair_grads(q_b[chunk_len:], do_b[chunk_len:], lse_b[chunk_len:], delta_sum[chunk_len:], k_blk[:chunk_len], v_blk[:chunk_len], None)
    dq_second, dk_second, dv_second = pair_grads(q_b[chunk_len:], do_b[chunk_len:], lse_b[chunk_len:], delta_sum[chunk_len:], k_blk[chunk_len:], v_blk[chunk_len:], tri_mask)
    dq_own = jnp.concatenate([dq_first, dq_cross + dq_second])
    dk_own = jnp.concatenate([dk_first + dk_cross, dk_second])
    dv_own = jnp.concatenate([dv_first + dv_cross, dv_second])
    return dq_own, dk_own, dv_own


def early_source(q_b, do_b, lse_b, delta_sum, k_blk, v_blk, dq_acc, dk_acc, dv_acc):
    chunk_len = k_blk.shape[0] // 2
    dq_part, dk_part, dv_part = pair_grads(q_b, do_b, lse_b, delta_sum, k_blk[:chunk_len], v_blk[:chunk_len], None)
    return (dq_acc + dq_part,
            jnp.concatenate([dk_acc[:chunk_len] + dk_part, dk_acc[chunk_len:]]),
            jnp.concatenate([dv_acc[:chunk_len] + dv_part, dv_acc[chunk_len:]]))


def late_source(q_b, do_b, lse_b, delta_sum, k_blk, v_blk, dq_acc, dk_acc, dv_acc):
    chunk_len = k_blk.shape[0] // 2
    dq_part, dk_part, dv_part = pair_grads(q_b[chunk_len:], do_b[chunk_len:], lse_b[chunk_len:], delta_sum[chunk_len:], k_blk, v_blk, None)
    return (jnp.concatenate([dq_acc[:chunk_len], dq_acc[chunk_len:] + dq_part]),
            dk_acc + dk_part,
            dv_acc + dv_part)


def solution(mesh):
    cp_size = mesh.shape['cp']
    shift_pairs = [(source, (source + 1) % cp_size) for source in range(cp_size)]

    def local_grads(q_raw, k_raw, v_proj, out_fwd, lse_fwd, d_out, q_norm, k_norm):
        dev_rank = lax.axis_index('cp')
        local_rows, num_heads = q_raw.shape[0], q_raw.shape[1]
        chunk_len = local_rows // 2
        kv_heads = k_raw.shape[1]
        per_kv = num_heads // kv_heads
        offsets = jnp.arange(chunk_len)
        positions = jnp.concatenate([dev_rank * chunk_len + offsets, (2 * cp_size - 1 - dev_rank) * chunk_len + offsets])
        cos_t, sin_t = rope_tables(positions)
        prepare = lambda raw_in, weight: norm_rope(raw_in, weight, cos_t, sin_t)
        q_full, pull_q = jax.vjp(prepare, q_raw.astype(jnp.float32), q_norm)
        k_full, pull_k = jax.vjp(prepare, k_raw.astype(jnp.float32), k_norm)
        q_b = q_full.astype(jnp.bfloat16).reshape(local_rows, kv_heads, per_kv, HEAD_DIM)
        k_b = k_full.astype(jnp.bfloat16)
        do_b = d_out.reshape(local_rows, kv_heads, per_kv, HEAD_DIM)
        lse_b = lse_fwd.reshape(local_rows, kv_heads, per_kv)
        delta_sum = jnp.einsum('thd,thd->th', d_out, out_fwd, preferred_element_type=jnp.float32).reshape(local_rows, kv_heads, per_kv)
        dq_acc, dk_acc, dv_acc = own_grads(q_b, do_b, lse_b, delta_sum, k_b, v_proj)

        def visit_source(step_idx, loop_state):
            k_cur, v_cur, dq_cur, dk_cur, dv_cur = loop_state
            k_cur = lax.ppermute(k_cur, 'cp', shift_pairs)
            v_cur = lax.ppermute(v_cur, 'cp', shift_pairs)
            dk_cur = lax.ppermute(dk_cur, 'cp', shift_pairs)
            dv_cur = lax.ppermute(dv_cur, 'cp', shift_pairs)
            source = (dev_rank - step_idx) % cp_size
            dq_cur, dk_cur, dv_cur = lax.cond(source < dev_rank, early_source, late_source, q_b, do_b, lse_b, delta_sum, k_cur, v_cur, dq_cur, dk_cur, dv_cur)
            return k_cur, v_cur, dq_cur, dk_cur, dv_cur

        loop_state = lax.fori_loop(1, cp_size, visit_source, (k_b, v_proj, dq_acc, dk_acc, dv_acc))
        dq_acc, dk_cur, dv_cur = loop_state[2], loop_state[3], loop_state[4]
        dk_home = lax.ppermute(dk_cur, 'cp', shift_pairs)
        dv_home = lax.ppermute(dv_cur, 'cp', shift_pairs)
        dq_raw, dq_weight = pull_q(dq_acc.reshape(local_rows, num_heads, HEAD_DIM))
        dk_raw, dk_weight = pull_k(dk_home)
        return (dq_raw.astype(jnp.bfloat16), dk_raw.astype(jnp.bfloat16), dv_home.astype(jnp.bfloat16),
                lax.psum(dq_weight, 'cp'), lax.psum(dk_weight, 'cp'))

    row_spec = P(('dp', 'cp'))
    in_specs = (row_spec, row_spec, row_spec, row_spec, row_spec, row_spec, P(), P())
    out_specs = (row_spec, row_spec, row_spec, P('dp'), P('dp'))
    return jax.shard_map(local_grads, mesh=mesh, in_specs=in_specs, out_specs=out_specs, check_vma=False)
```

profile of v0, /device:TPU:81, one launch (start us, length us, event | category | flops | bytes accessed | tf_op | source)
XLA Modules:
  0.0 1165.7 jit_solution(560565450100000626)
XLA Ops:
  143.3 930.0 %while.23 = (s32[]{:T(128)}, bf16[512,8,128]{2,0,1:T(8,128)(2,1)}, bf16[512,8,128]{2,0,1:T(8,128)(2,1)}, f32[512,8,4,128]{3,0,2,1:T(8,128)}, f32[512,8,128]{2,0,...) while((s32[]{:T(128)}, bf16[512,8,128]{2,0,1:T(8,128)(2,1)}, ...), condition=%wide.region_5.6_spmd, body=%wide.region_2.5_spmd.sunk | while | flops 5408292864 | bytes 220136208 | solution.py:102
  148.0 54.9 %collective-permute-done.1 = bf16[512,8,128]{2,0,1:T(8,128)(2,1)S(1)} collective-permute-done((bf16[512,8,128]{2,0,1:T(8,128)(2,1)}, bf16[512,8,128]{2,0,1:T(8,128)(2,1)S(1)}, u32[]{:S(2)}, u32[]{:S(2)}) %collective-permute-start.1) | collective-permute-done | bytes 1048608 | tf_op jit(solution)/shard_map/while/body/eval_jaxpr/ppermute | solution.py:95
  215.0 59.9 %conditional.2 = (f32[512,8,4,128]{3,0,2,1:T(8,128)}, f32[512,8,128]{2,0,1:T(8,128)}, f32[512,8,128]{2,0,1:T(8,128)}) conditional(s32[]{:T(128)} %convert_element_type.164, (f32[512,8,4,128]{3,0,2,1:T(8,128)}, bf16[512,8,4,128]{3,0,2,1:T(8,128)(2,1)}, bf16[512,8,128]{2,0,1:T(8,128)(2,1)S(1)}, f32[512,8,4]{0,2,1:T(4,128)S(1)}, ...), branch_computations={%region_3.3_spmd, %region_4.4_spmd} | conditional | flops 5408292864 | bytes 190775488 | solution.py:99
  219.7 10.5 fusion.43
  259.1 12.2 %bitcast_add_fusion.3 = f32[512,8,4,128]{3,0,2,1:T(8,128)} fusion(f32[512,8,4,128]{3,0,2,1:T(8,128)} %get-tuple-element.354, bf16[512,8,4,256]{0,3,2,1:T(8,128)(2,1)} %copy-done, bf16[512,8,128]{2,0,1:T(8,128)(2,1)S(1)} %get-tuple-element.355), kind=kOutput, calls=%fused_computation.31 | convolution fusion | flops 1077936128 | bytes 25690112 | tf_op jit(solution)/shard_map/while/body/eval_jaxpr/cond/branch_1_fun/qngk,knd->qngd/dot_general | solution.py:35
  279.2 54.9 %collective-permute-done.1 = bf16[512,8,128]{2,0,1:T(8,128)(2,1)S(1)} collective-permute-done((bf16[512,8,128]{2,0,1:T(8,128)(2,1)}, bf16[512,8,128]{2,0,1:T(8,128)(2,1)S(1)}, u32[]{:S(2)}, u32[]{:S(2)}) %collective-permute-start.1) | collective-permute-done | bytes 1048608 | tf_op jit(solution)/shard_map/while/body/eval_jaxpr/ppermute | solution.py:95
  346.4 60.6 %conditional.2 = (f32[512,8,4,128]{3,0,2,1:T(8,128)}, f32[512,8,128]{2,0,1:T(8,128)}, f32[512,8,128]{2,0,1:T(8,128)}) conditional(s32[]{:T(128)} %convert_element_type.164, (f32[512,8,4,128]{3,0,2,1:T(8,128)}, bf16[512,8,4,128]{3,0,2,1:T(8,128)(2,1)}, bf16[512,8,128]{2,0,1:T(8,128)(2,1)S(1)}, f32[512,8,4]{0,2,1:T(4,128)S(1)}, ...), branch_computations={%region_3.3_spmd, %region_4.4_spmd} | conditional | flops 5408292864 | bytes 190775488 | solution.py:99
  360.8 11.4 bitcast_add_fusion.1
  372.2 10.6 fusion.1
  410.5 54.9 %collective-permute-done.1 = bf16[512,8,128]{2,0,1:T(8,128)(2,1)S(1)} collective-permute-done((bf16[512,8,128]{2,0,1:T(8,128)(2,1)}, bf16[512,8,128]{2,0,1:T(8,128)(2,1)S(1)}, u32[]{:S(2)}, u32[]{:S(2)}) %collective-permute-start.1) | collective-permute-done | bytes 1048608 | tf_op jit(solution)/shard_map/while/body/eval_jaxpr/ppermute | solution.py:95
  477.7 60.6 %conditional.2 = (f32[512,8,4,128]{3,0,2,1:T(8,128)}, f32[512,8,128]{2,0,1:T(8,128)}, f32[512,8,128]{2,0,1:T(8,128)}) conditional(s32[]{:T(128)} %convert_element_type.164, (f32[512,8,4,128]{3,0,2,1:T(8,128)}, bf16[512,8,4,128]{3,0,2,1:T(8,128)(2,1)}, bf16[512,8,128]{2,0,1:T(8,128)(2,1)S(1)}, f32[512,8,4]{0,2,1:T(4,128)S(1)}, ...), branch_computations={%region_3.3_spmd, %region_4.4_spmd} | conditional | flops 5408292864 | bytes 190775488 | solution.py:99
  492.1 11.4 bitcast_add_fusion.1
  503.5 10.6 fusion.1
  541.9 55.5 %collective-permute-done.1 = bf16[512,8,128]{2,0,1:T(8,128)(2,1)S(1)} collective-permute-done((bf16[512,8,128]{2,0,1:T(8,128)(2,1)}, bf16[512,8,128]{2,0,1:T(8,128)(2,1)S(1)}, u32[]{:S(2)}, u32[]{:S(2)}) %collective-permute-start.1) | collective-permute-done | bytes 1048608 | tf_op jit(solution)/shard_map/while/body/eval_jaxpr/ppermute | solution.py:95
  609.6 60.6 %conditional.2 = (f32[512,8,4,128]{3,0,2,1:T(8,128)}, f32[512,8,128]{2,0,1:T(8,128)}, f32[512,8,128]{2,0,1:T(8,128)}) conditional(s32[]{:T(128)} %convert_element_type.164, (f32[512,8,4,128]{3,0,2,1:T(8,128)}, bf16[512,8,4,128]{3,0,2,1:T(8,128)(2,1)}, bf16[512,8,128]{2,0,1:T(8,128)(2,1)S(1)}, f32[512,8,4]{0,2,1:T(4,128)S(1)}, ...), branch_computations={%region_3.3_spmd, %region_4.4_spmd} | conditional | flops 5408292864 | bytes 190775488 | solution.py:99
  624.1 11.4 bitcast_add_fusion.1
  635.5 10.6 fusion.1
  673.2 56.2 %collective-permute-done.1 = bf16[512,8,128]{2,0,1:T(8,128)(2,1)S(1)} collective-permute-done((bf16[512,8,128]{2,0,1:T(8,128)(2,1)}, bf16[512,8,128]{2,0,1:T(8,128)(2,1)S(1)}, u32[]{:S(2)}, u32[]{:S(2)}) %collective-permute-start.1) | collective-permute-done | bytes 1048608 | tf_op jit(solution)/shard_map/while/body/eval_jaxpr/ppermute | solution.py:95
  741.6 60.6 %conditional.2 = (f32[512,8,4,128]{3,0,2,1:T(8,128)}, f32[512,8,128]{2,0,1:T(8,128)}, f32[512,8,128]{2,0,1:T(8,128)}) conditional(s32[]{:T(128)} %convert_element_type.164, (f32[512,8,4,128]{3,0,2,1:T(8,128)}, bf16[512,8,4,128]{3,0,2,1:T(8,128)(2,1)}, bf16[512,8,128]{2,0,1:T(8,128)(2,1)S(1)}, f32[512,8,4]{0,2,1:T(4,128)S(1)}, ...), branch_computations={%region_3.3_spmd, %region_4.4_spmd} | conditional | flops 5408292864 | bytes 190775488 | solution.py:99
  756.0 11.4 bitcast_add_fusion.1
  767.4 10.6 fusion.1
  805.1 56.2 %collective-permute-done.1 = bf16[512,8,128]{2,0,1:T(8,128)(2,1)S(1)} collective-permute-done((bf16[512,8,128]{2,0,1:T(8,128)(2,1)}, bf16[512,8,128]{2,0,1:T(8,128)(2,1)S(1)}, u32[]{:S(2)}, u32[]{:S(2)}) %collective-permute-start.1) | collective-permute-done | bytes 1048608 | tf_op jit(solution)/shard_map/while/body/eval_jaxpr/ppermute | solution.py:95
  873.5 60.6 %conditional.2 = (f32[512,8,4,128]{3,0,2,1:T(8,128)}, f32[512,8,128]{2,0,1:T(8,128)}, f32[512,8,128]{2,0,1:T(8,128)}) conditional(s32[]{:T(128)} %convert_element_type.164, (f32[512,8,4,128]{3,0,2,1:T(8,128)}, bf16[512,8,4,128]{3,0,2,1:T(8,128)(2,1)}, bf16[512,8,128]{2,0,1:T(8,128)(2,1)S(1)}, f32[512,8,4]{0,2,1:T(4,128)S(1)}, ...), branch_computations={%region_3.3_spmd, %region_4.4_spmd} | conditional | flops 5408292864 | bytes 190775488 | solution.py:99
  888.0 11.4 bitcast_add_fusion.1
  899.4 10.6 fusion.1
  937.1 56.2 %collective-permute-done.1 = bf16[512,8,128]{2,0,1:T(8,128)(2,1)S(1)} collective-permute-done((bf16[512,8,128]{2,0,1:T(8,128)(2,1)}, bf16[512,8,128]{2,0,1:T(8,128)(2,1)S(1)}, u32[]{:S(2)}, u32[]{:S(2)}) %collective-permute-start.1) | collective-permute-done | bytes 1048608 | tf_op jit(solution)/shard_map/while/body/eval_jaxpr/ppermute | solution.py:95
  1005.5 60.6 %conditional.2 = (f32[512,8,4,128]{3,0,2,1:T(8,128)}, f32[512,8,128]{2,0,1:T(8,128)}, f32[512,8,128]{2,0,1:T(8,128)}) conditional(s32[]{:T(128)} %convert_element_type.164, (f32[512,8,4,128]{3,0,2,1:T(8,128)}, bf16[512,8,4,128]{3,0,2,1:T(8,128)(2,1)}, bf16[512,8,128]{2,0,1:T(8,128)(2,1)S(1)}, f32[512,8,4]{0,2,1:T(4,128)S(1)}, ...), branch_computations={%region_3.3_spmd, %region_4.4_spmd} | conditional | flops 5408292864 | bytes 190775488 | solution.py:99
  1019.9 11.4 bitcast_add_fusion.1
  1031.3 10.6 fusion.1
  1079.6 12.1 %copy.101 = f32[512,8,4,128]{3,2,1,0:T(4,128)} copy(f32[512,8,4,128]{3,0,2,1:T(8,128)} %get-tuple-element.388) | data formatting | bytes 16777216 | tf_op jit(solution)/shard_map/while | solution.py:102
  1104.6 18.3 %fusion.51 = (f32[128]{0:T(128)S(1)}, f32[512,32]{1,0:T(8,128)S(1)}, f32[512,32,128]{2,1,0:T(8,128)}) fusion(bf16[512,32,128]{2,1,0:T(8,128)(2,1)S(1)} %copy-done.3, f32[512,32]{1,0:T(8,128)S(1)} %copy-done.19, f32[128]{0:T(128)S(1)} %copy-done.46, f32[512,32,64]{2,1,0:T(8,128)} %get-tuple-element.482, f32[512,32,64]{2,1,0:T(8,128)} %get-tuple-element.481, ...), kind=kLoop, calls=%fused_computation.57 | loop fusion | flops 20955008 | bytes 29754368 | tf_op jit(solution)/shard_map/transpose(jvp())/reduce_sum | solution.py:20
  1141.3 21.9 %all-reduce.4 = (f32[128]{0:T(128)}, f32[128]{0:T(128)}) all-reduce(f32[128]{0:T(128)S(1)} %get-tuple-element.445, f32[128]{0:T(128)S(1)} %get-tuple-element.447), channel_id=1, replica_groups=mesh['dp'=4,'cp'=8] {'cp'}, use_global_device_ids=true, to_apply=%region_9.10 | all-reduce | flops 256 | bytes 2048 | tf_op jit(solution)/shard_map/psum | solution.py:109
  (327 shorter events, 561.2 us)
Async XLA Ops:
  20.0 32.1 %copy-start.33 = (f32[512,8]{0,1:T(8,128)}, f32[512,8]{0,1:T(8,128)S(1)}, u32[]{:S(2)}) copy-start(f32[512,8]{0,1:T(8,128)S(1)} %fusion.123) | copy-start | bytes 49156
  143.4 71.6 %collective-permute-start.3 = (f32[512,8,128]{2,0,1:T(8,128)}, f32[512,8,128]{2,0,1:T(8,128)}, u32[]{:S(2)}, u32[]{:S(2)}) collective-permute-start(f32[512,8,128]{2,0,1:T(8,128)} %get-tuple-element.614), channel_id=1, source_target_pairs={{0,1},{1,2},{2,3},{3,4},{4,5},{5,6},{6,7},{7,0},{8,9},{9,10},{10,1... | collective-permute-start | bytes 6291464 | tf_op jit(solution)/shard_map/while/body/eval_jaxpr/ppermute | solution.py:97
  146.2 68.9 %collective-permute-start.2 = (f32[512,8,128]{2,0,1:T(8,128)}, f32[512,8,128]{2,0,1:T(8,128)}, u32[]{:S(2)}, u32[]{:S(2)}) collective-permute-start(f32[512,8,128]{2,0,1:T(8,128)} %get-tuple-element.613), channel_id=1, source_target_pairs={{0,1},{1,2},{2,3},{3,4},{4,5},{5,6},{6,7},{7,0},{8,9},{9,10},{10,1... | collective-permute-start | bytes 6291464 | tf_op jit(solution)/shard_map/while/body/eval_jaxpr/ppermute | solution.py:96
  146.2 56.6 %collective-permute-start.1 = (bf16[512,8,128]{2,0,1:T(8,128)(2,1)}, bf16[512,8,128]{2,0,1:T(8,128)(2,1)S(1)}, u32[]{:S(2)}, u32[]{:S(2)}) collective-permute-start(bf16[512,8,128]{2,0,1:T(8,128)(2,1)} %get-tuple-element.611), channel_id=1, source_target_pairs={{0,1},{1,2},{2,3},{3,4},{4,5},{5,6},{6,7},{7,0},{8,9},{9,10},{10,1... | collective-permute-start | bytes 3145736 | tf_op jit(solution)/shard_map/while/body/eval_jaxpr/ppermute | solution.py:95
  147.9 66.2 %collective-permute-start = (bf16[512,8,128]{2,0,1:T(8,128)(2,1)}, bf16[512,8,128]{2,0,1:T(8,128)(2,1)S(1)}, u32[]{:S(2)}, u32[]{:S(2)}) collective-permute-start(bf16[512,8,128]{2,0,1:T(8,128)(2,1)} %get-tuple-element.610), channel_id=1, source_target_pairs={{0,1},{1,2},{2,3},{3,4},{4,5},{5,6},{6,7},{7,0},{8,9},{9,10},{10,1... | collective-permute-start | bytes 3145736 | tf_op jit(solution)/shard_map/while/body/eval_jaxpr/ppermute | solution.py:94
  275.0 71.4 %collective-permute-start.3 = (f32[512,8,128]{2,0,1:T(8,128)}, f32[512,8,128]{2,0,1:T(8,128)}, u32[]{:S(2)}, u32[]{:S(2)}) collective-permute-start(f32[512,8,128]{2,0,1:T(8,128)} %get-tuple-element.614), channel_id=1, source_target_pairs={{0,1},{1,2},{2,3},{3,4},{4,5},{5,6},{6,7},{7,0},{8,9},{9,10},{10,1... | collective-permute-start | bytes 6291464 | tf_op jit(solution)/shard_map/while/body/eval_jaxpr/ppermute | solution.py:97
  277.5 68.9 %collective-permute-start.2 = (f32[512,8,128]{2,0,1:T(8,128)}, f32[512,8,128]{2,0,1:T(8,128)}, u32[]{:S(2)}, u32[]{:S(2)}) collective-permute-start(f32[512,8,128]{2,0,1:T(8,128)} %get-tuple-element.613), channel_id=1, source_target_pairs={{0,1},{1,2},{2,3},{3,4},{4,5},{5,6},{6,7},{7,0},{8,9},{9,10},{10,1... | collective-permute-start | bytes 6291464 | tf_op jit(solution)/shard_map/while/body/eval_jaxpr/ppermute | solution.py:96
  277.5 56.6 %collective-permute-start.1 = (bf16[512,8,128]{2,0,1:T(8,128)(2,1)}, bf16[512,8,128]{2,0,1:T(8,128)(2,1)S(1)}, u32[]{:S(2)}, u32[]{:S(2)}) collective-permute-start(bf16[512,8,128]{2,0,1:T(8,128)(2,1)} %get-tuple-element.611), channel_id=1, source_target_pairs={{0,1},{1,2},{2,3},{3,4},{4,5},{5,6},{6,7},{7,0},{8,9},{9,10},{10,1... | collective-permute-start | bytes 3145736 | tf_op jit(solution)/shard_map/while/body/eval_jaxpr/ppermute | solution.py:95
  279.2 66.2 %collective-permute-start = (bf16[512,8,128]{2,0,1:T(8,128)(2,1)}, bf16[512,8,128]{2,0,1:T(8,128)(2,1)S(1)}, u32[]{:S(2)}, u32[]{:S(2)}) collective-permute-start(bf16[512,8,128]{2,0,1:T(8,128)(2,1)} %get-tuple-element.610), channel_id=1, source_target_pairs={{0,1},{1,2},{2,3},{3,4},{4,5},{5,6},{6,7},{7,0},{8,9},{9,10},{10,1... | collective-permute-start | bytes 3145736 | tf_op jit(solution)/shard_map/while/body/eval_jaxpr/ppermute | solution.py:94
  360.8 30.2 %slice-start = ((s8[8388608]{0:T(1024)(128)(4,1)}), s8[4194304]{0:T(1024)(128)(4,1)S(1)}, s32[]{:S(2)}) async-start(s8[8388608]{0:T(1024)(128)(4,1)} %bitcast.286), calls=%async_computation | async-start | bytes 8388608 | tf_op jit(solution)/shard_map/while/body/eval_jaxpr/cond
  406.9 70.7 %collective-permute-start.3 = (f32[512,8,128]{2,0,1:T(8,128)}, f32[512,8,128]{2,0,1:T(8,128)}, u32[]{:S(2)}, u32[]{:S(2)}) collective-permute-start(f32[512,8,128]{2,0,1:T(8,128)} %get-tuple-element.614), channel_id=1, source_target_pairs={{0,1},{1,2},{2,3},{3,4},{4,5},{5,6},{6,7},{7,0},{8,9},{9,10},{10,1... | collective-permute-start | bytes 6291464 | tf_op jit(solution)/shard_map/while/body/eval_jaxpr/ppermute | solution.py:97
  408.8 68.9 %collective-permute-start.2 = (f32[512,8,128]{2,0,1:T(8,128)}, f32[512,8,128]{2,0,1:T(8,128)}, u32[]{:S(2)}, u32[]{:S(2)}) collective-permute-start(f32[512,8,128]{2,0,1:T(8,128)} %get-tuple-element.613), channel_id=1, source_target_pairs={{0,1},{1,2},{2,3},{3,4},{4,5},{5,6},{6,7},{7,0},{8,9},{9,10},{10,1... | collective-permute-start | bytes 6291464 | tf_op jit(solution)/shard_map/while/body/eval_jaxpr/ppermute | solution.py:96
  408.8 56.6 %collective-permute-start.1 = (bf16[512,8,128]{2,0,1:T(8,128)(2,1)}, bf16[512,8,128]{2,0,1:T(8,128)(2,1)S(1)}, u32[]{:S(2)}, u32[]{:S(2)}) collective-permute-start(bf16[512,8,128]{2,0,1:T(8,128)(2,1)} %get-tuple-element.611), channel_id=1, source_target_pairs={{0,1},{1,2},{2,3},{3,4},{4,5},{5,6},{6,7},{7,0},{8,9},{9,10},{10,1... | collective-permute-start | bytes 3145736 | tf_op jit(solution)/shard_map/while/body/eval_jaxpr/ppermute | solution.py:95
  410.5 66.2 %collective-permute-start = (bf16[512,8,128]{2,0,1:T(8,128)(2,1)}, bf16[512,8,128]{2,0,1:T(8,128)(2,1)S(1)}, u32[]{:S(2)}, u32[]{:S(2)}) collective-permute-start(bf16[512,8,128]{2,0,1:T(8,128)(2,1)} %get-tuple-element.610), channel_id=1, source_target_pairs={{0,1},{1,2},{2,3},{3,4},{4,5},{5,6},{6,7},{7,0},{8,9},{9,10},{10,1... | collective-permute-start | bytes 3145736 | tf_op jit(solution)/shard_map/while/body/eval_jaxpr/ppermute | solution.py:94
  538.2 71.4 %collective-permute-start.3 = (f32[512,8,128]{2,0,1:T(8,128)}, f32[512,8,128]{2,0,1:T(8,128)}, u32[]{:S(2)}, u32[]{:S(2)}) collective-permute-start(f32[512,8,128]{2,0,1:T(8,128)} %get-tuple-element.614), channel_id=1, source_target_pairs={{0,1},{1,2},{2,3},{3,4},{4,5},{5,6},{6,7},{7,0},{8,9},{9,10},{10,1... | collective-permute-start | bytes 6291464 | tf_op jit(solution)/shard_map/while/body/eval_jaxpr/ppermute | solution.py:97
  540.7 68.9 %collective-permute-start.2 = (f32[512,8,128]{2,0,1:T(8,128)}, f32[512,8,128]{2,0,1:T(8,128)}, u32[]{:S(2)}, u32[]{:S(2)}) collective-permute-start(f32[512,8,128]{2,0,1:T(8,128)} %get-tuple-element.613), channel_id=1, source_target_pairs={{0,1},{1,2},{2,3},{3,4},{4,5},{5,6},{6,7},{7,0},{8,9},{9,10},{10,1... | collective-permute-start | bytes 6291464 | tf_op jit(solution)/shard_map/while/body/eval_jaxpr/ppermute | solution.py:96
  540.7 56.6 %collective-permute-start.1 = (bf16[512,8,128]{2,0,1:T(8,128)(2,1)}, bf16[512,8,128]{2,0,1:T(8,128)(2,1)S(1)}, u32[]{:S(2)}, u32[]{:S(2)}) collective-permute-start(bf16[512,8,128]{2,0,1:T(8,128)(2,1)} %get-tuple-element.611), channel_id=1, source_target_pairs={{0,1},{1,2},{2,3},{3,4},{4,5},{5,6},{6,7},{7,0},{8,9},{9,10},{10,1... | collective-permute-start | bytes 3145736 | tf_op jit(solution)/shard_map/while/body/eval_jaxpr/ppermute | solution.py:95
  541.8 66.8 %collective-permute-start = (bf16[512,8,128]{2,0,1:T(8,128)(2,1)}, bf16[512,8,128]{2,0,1:T(8,128)(2,1)S(1)}, u32[]{:S(2)}, u32[]{:S(2)}) collective-permute-start(bf16[512,8,128]{2,0,1:T(8,128)(2,1)} %get-tuple-element.610), channel_id=1, source_target_pairs={{0,1},{1,2},{2,3},{3,4},{4,5},{5,6},{6,7},{7,0},{8,9},{9,10},{10,1... | collective-permute-start | bytes 3145736 | tf_op jit(solution)/shard_map/while/body/eval_jaxpr/ppermute | solution.py:94
  670.2 71.4 %collective-permute-start.3 = (f32[512,8,128]{2,0,1:T(8,128)}, f32[512,8,128]{2,0,1:T(8,128)}, u32[]{:S(2)}, u32[]{:S(2)}) collective-permute-start(f32[512,8,128]{2,0,1:T(8,128)} %get-tuple-element.614), channel_id=1, source_target_pairs={{0,1},{1,2},{2,3},{3,4},{4,5},{5,6},{6,7},{7,0},{8,9},{9,10},{10,1... | collective-permute-start | bytes 6291464 | tf_op jit(solution)/shard_map/while/body/eval_jaxpr/ppermute | solution.py:97
  672.7 68.9 %collective-permute-start.2 = (f32[512,8,128]{2,0,1:T(8,128)}, f32[512,8,128]{2,0,1:T(8,128)}, u32[]{:S(2)}, u32[]{:S(2)}) collective-permute-start(f32[512,8,128]{2,0,1:T(8,128)} %get-tuple-element.613), channel_id=1, source_target_pairs={{0,1},{1,2},{2,3},{3,4},{4,5},{5,6},{6,7},{7,0},{8,9},{9,10},{10,1... | collective-permute-start | bytes 6291464 | tf_op jit(solution)/shard_map/while/body/eval_jaxpr/ppermute | solution.py:96
  672.7 56.6 %collective-permute-start.1 = (bf16[512,8,128]{2,0,1:T(8,128)(2,1)}, bf16[512,8,128]{2,0,1:T(8,128)(2,1)S(1)}, u32[]{:S(2)}, u32[]{:S(2)}) collective-permute-start(bf16[512,8,128]{2,0,1:T(8,128)(2,1)} %get-tuple-element.611), channel_id=1, source_target_pairs={{0,1},{1,2},{2,3},{3,4},{4,5},{5,6},{6,7},{7,0},{8,9},{9,10},{10,1... | collective-permute-start | bytes 3145736 | tf_op jit(solution)/shard_map/while/body/eval_jaxpr/ppermute | solution.py:95
  673.1 67.4 %collective-permute-start = (bf16[512,8,128]{2,0,1:T(8,128)(2,1)}, bf16[512,8,128]{2,0,1:T(8,128)(2,1)S(1)}, u32[]{:S(2)}, u32[]{:S(2)}) collective-permute-start(bf16[512,8,128]{2,0,1:T(8,128)(2,1)} %get-tuple-element.610), channel_id=1, source_target_pairs={{0,1},{1,2},{2,3},{3,4},{4,5},{5,6},{6,7},{7,0},{8,9},{9,10},{10,1... | collective-permute-start | bytes 3145736 | tf_op jit(solution)/shard_map/while/body/eval_jaxpr/ppermute | solution.py:94
  802.1 71.4 %collective-permute-start.3 = (f32[512,8,128]{2,0,1:T(8,128)}, f32[512,8,128]{2,0,1:T(8,128)}, u32[]{:S(2)}, u32[]{:S(2)}) collective-permute-start(f32[512,8,128]{2,0,1:T(8,128)} %get-tuple-element.614), channel_id=1, source_target_pairs={{0,1},{1,2},{2,3},{3,4},{4,5},{5,6},{6,7},{7,0},{8,9},{9,10},{10,1... | collective-permute-start | bytes 6291464 | tf_op jit(solution)/shard_map/while/body/eval_jaxpr/ppermute | solution.py:97
  804.6 68.9 %collective-permute-start.2 = (f32[512,8,128]{2,0,1:T(8,128)}, f32[512,8,128]{2,0,1:T(8,128)}, u32[]{:S(2)}, u32[]{:S(2)}) collective-permute-start(f32[512,8,128]{2,0,1:T(8,128)} %get-tuple-element.613), channel_id=1, source_target_pairs={{0,1},{1,2},{2,3},{3,4},{4,5},{5,6},{6,7},{7,0},{8,9},{9,10},{10,1... | collective-permute-start | bytes 6291464 | tf_op jit(solution)/shard_map/while/body/eval_jaxpr/ppermute | solution.py:96
  804.6 56.6 %collective-permute-start.1 = (bf16[512,8,128]{2,0,1:T(8,128)(2,1)}, bf16[512,8,128]{2,0,1:T(8,128)(2,1)S(1)}, u32[]{:S(2)}, u32[]{:S(2)}) collective-permute-start(bf16[512,8,128]{2,0,1:T(8,128)(2,1)} %get-tuple-element.611), channel_id=1, source_target_pairs={{0,1},{1,2},{2,3},{3,4},{4,5},{5,6},{6,7},{7,0},{8,9},{9,10},{10,1... | collective-permute-start | bytes 3145736 | tf_op jit(solution)/shard_map/while/body/eval_jaxpr/ppermute | solution.py:95
  805.1 67.4 %collective-permute-start = (bf16[512,8,128]{2,0,1:T(8,128)(2,1)}, bf16[512,8,128]{2,0,1:T(8,128)(2,1)S(1)}, u32[]{:S(2)}, u32[]{:S(2)}) collective-permute-start(bf16[512,8,128]{2,0,1:T(8,128)(2,1)} %get-tuple-element.610), channel_id=1, source_target_pairs={{0,1},{1,2},{2,3},{3,4},{4,5},{5,6},{6,7},{7,0},{8,9},{9,10},{10,1... | collective-permute-start | bytes 3145736 | tf_op jit(solution)/shard_map/while/body/eval_jaxpr/ppermute | solution.py:94
  934.1 71.4 %collective-permute-start.3 = (f32[512,8,128]{2,0,1:T(8,128)}, f32[512,8,128]{2,0,1:T(8,128)}, u32[]{:S(2)}, u32[]{:S(2)}) collective-permute-start(f32[512,8,128]{2,0,1:T(8,128)} %get-tuple-element.614), channel_id=1, source_target_pairs={{0,1},{1,2},{2,3},{3,4},{4,5},{5,6},{6,7},{7,0},{8,9},{9,10},{10,1... | collective-permute-start | bytes 6291464 | tf_op jit(solution)/shard_map/while/body/eval_jaxpr/ppermute | solution.py:97
  936.6 68.9 %collective-permute-start.2 = (f32[512,8,128]{2,0,1:T(8,128)}, f32[512,8,128]{2,0,1:T(8,128)}, u32[]{:S(2)}, u32[]{:S(2)}) collective-permute-start(f32[512,8,128]{2,0,1:T(8,128)} %get-tuple-element.613), channel_id=1, source_target_pairs={{0,1},{1,2},{2,3},{3,4},{4,5},{5,6},{6,7},{7,0},{8,9},{9,10},{10,1... | collective-permute-start | bytes 6291464 | tf_op jit(solution)/shard_map/while/body/eval_jaxpr/ppermute | solution.py:96
  936.6 56.6 %collective-permute-start.1 = (bf16[512,8,128]{2,0,1:T(8,128)(2,1)}, bf16[512,8,128]{2,0,1:T(8,128)(2,1)S(1)}, u32[]{:S(2)}, u32[]{:S(2)}) collective-permute-start(bf16[512,8,128]{2,0,1:T(8,128)(2,1)} %get-tuple-element.611), channel_id=1, source_target_pairs={{0,1},{1,2},{2,3},{3,4},{4,5},{5,6},{6,7},{7,0},{8,9},{9,10},{10,1... | collective-permute-start | bytes 3145736 | tf_op jit(solution)/shard_map/while/body/eval_jaxpr/ppermute | solution.py:95
  937.0 67.4 %collective-permute-start = (bf16[512,8,128]{2,0,1:T(8,128)(2,1)}, bf16[512,8,128]{2,0,1:T(8,128)(2,1)S(1)}, u32[]{:S(2)}, u32[]{:S(2)}) collective-permute-start(bf16[512,8,128]{2,0,1:T(8,128)(2,1)} %get-tuple-element.610), channel_id=1, source_target_pairs={{0,1},{1,2},{2,3},{3,4},{4,5},{5,6},{6,7},{7,0},{8,9},{9,10},{10,1... | collective-permute-start | bytes 3145736 | tf_op jit(solution)/shard_map/while/body/eval_jaxpr/ppermute | solution.py:94
  1077.1 55.2 %collective-permute-start.5 = (bf16[512,8,128]{2,1,0:T(8,128)(2,1)}, bf16[512,8,128]{2,1,0:T(8,128)(2,1)}, u32[]{:S(2)}, u32[]{:S(2)}) collective-permute-start(bf16[512,8,128]{2,1,0:T(8,128)(2,1)} %copy.104), channel_id=1, source_target_pairs={{0,1},{1,2},{2,3},{3,4},{4,5},{5,6},{6,7},{7,0},{8,9},{9,10},{10,1... | collective-permute-start | bytes 3145736 | tf_op jit(solution)/shard_map/ppermute | solution.py:105
  1079.6 52.7 %collective-permute-start.4 = (f32[512,8,128]{2,0,1:T(8,128)}, f32[512,8,128]{2,0,1:T(8,128)}, u32[]{:S(2)}, u32[]{:S(2)}) collective-permute-start(f32[512,8,128]{2,0,1:T(8,128)} %get-tuple-element.389), channel_id=1, source_target_pairs={{0,1},{1,2},{2,3},{3,4},{4,5},{5,6},{6,7},{7,0},{8,9},{9,10},{10,1... | collective-permute-start | bytes 6291464 | tf_op jit(solution)/shard_map/ppermute | solution.py:104
  (63 other events, 554.7 us)
where the time goes:
time: 1170 us
  waiting for transfers between devices  461 us (39%)
  matrix products  392 us (34%)
  other arithmetic  141 us (12%)
  local copies, waits for them, and re-layouts  113 us (10%)
  starting transfers between devices  27.5 us (2%)
  blocking collectives  21.9 us (2%)
    ppermute x7, waiting for transfers between devices, visit_source(): v_cur = lax.ppermute(v_cur, 'cp', shift_pairs)  389 us
    dot_general x10, matrix products, pair_grads(): jnp.einsum('qngk,qngd->knd', prob_bf, do_blk, preferred_element_type=jnp....  90.7 us
    dot_general x10, matrix products, pair_grads(): jnp.einsum('qngd,knd->qngk', do_blk, v_blk, preferred_element_type=jnp.fl...  84.9 us
    dot_general x10, matrix products, pair_grads(): jnp.einsum('qngd,knd->qngk', q_blk, k_blk, preferred_element_type=jnp.flo...  82.8 us
    ppermute x7, waiting for transfers between devices, visit_source(): k_cur = lax.ppermute(k_cur, 'cp', shift_pairs)  71.9 us
    dot_general x10, matrix products, pair_grads(): jnp.einsum('qngk,knd->qngd', score_grad, k_blk, preferred_element_type=jn...  71.6 us
    dot_general x10, matrix products, pair_grads(): jnp.einsum('qngk,qngd->knd', score_grad, q_blk, preferred_element_type=jn...  61.8 us
    concatenate x6, other arithmetic, late_source(): jnp.concatenate([dq_acc[:chunk_len], dq_acc[chunk_len:] + dq_part])  46.1 us
  transfers between devices with their start and end apart: 30, of which 14 were waited for; matrix products, arithmetic and copies ran while one was open for 6% of the time, Pallas kernels for 0%

commit v1 on v0

v1 whole, which is shorter than its diff:
```python
import functools

import jax
import jax.numpy as jnp
from jax import lax
from jax.experimental import pallas as pl
from jax.experimental.pallas import tpu as pltpu
from jax.sharding import PartitionSpec as P

HEAD_DIM = 128
ROPE_THETA = 1000000.0
NORM_EPS = 1e-6
LOG2E = 1.4426950408889634
SM_SCALE = HEAD_DIM ** -0.5
CORES = 2


def rope_tables(positions):
    inv_freq = ROPE_THETA ** (-jnp.arange(0, HEAD_DIM, 2).astype(jnp.float32) / HEAD_DIM)
    angles = positions.astype(jnp.float32)[..., None] * inv_freq
    angles = jnp.concatenate([angles, angles], axis=-1)
    return jnp.cos(angles), jnp.sin(angles)


def norm_rope(raw_in, weight, cos_t, sin_t):
    mean_sq = jnp.mean(raw_in * raw_in, axis=-1, keepdims=True)
    normed = raw_in * lax.rsqrt(mean_sq + NORM_EPS) * weight
    half_dim = raw_in.shape[-1] // 2
    rotated = jnp.concatenate([-normed[..., half_dim:], normed[..., :half_dim]], axis=-1)
    return normed * cos_t + rotated * sin_t


def dot(a, b, dims):
    return lax.dot_general(a, b, (dims, ((), ())), preferred_element_type=jnp.float32)


def attn_kernel(chunk_len, per_kv, q_ref, do_ref, st_ref, k_ref, v_ref, dq_ref, dk_ref, dv_ref,
                qt_scr, dot_scr, dqt_scr, kt_scr, p_scr, ds_scr):
    chip = lax.axis_index('cp') // CORES
    num_src, num_chunks = k_ref.shape[0], k_ref.shape[2]
    for qb in range(num_chunks):
        qt_scr[qb] = q_ref[0, qb].T
        dot_scr[qb] = do_ref[0, qb].T
    dqt_scr[...] = jnp.zeros_like(dqt_scr)
    dk_ref[...] = jnp.zeros_like(dk_ref)
    dv_ref[...] = jnp.zeros_like(dv_ref)

    def block(src, kc, qb, masked):
        k_blk, v_blk = k_ref[src, 0, kc], v_ref[src, 0, kc]
        if masked:
            key_pos = lax.broadcasted_iota(jnp.int32, (chunk_len, chunk_len), 0)
            query_pos = lax.broadcasted_iota(jnp.int32, (chunk_len, chunk_len), 1)
            visible = key_pos <= query_pos
        for g in range(per_kv):
            cols = pl.ds(g * chunk_len, chunk_len)
            logits = dot(k_blk, qt_scr[qb, :, cols], ((1,), (0,))) * (SM_SCALE * LOG2E) - st_ref[0, qb, 0:1, cols]
            if masked:
                logits = jnp.where(visible, logits, -jnp.inf)
            prob = jnp.exp2(logits)
            dprob = dot(v_blk, dot_scr[qb, :, cols], ((1,), (0,)))
            p_scr[:, cols] = prob.astype(jnp.bfloat16)
            ds_scr[:, cols] = (prob * (dprob - st_ref[0, qb, 1:2, cols])).astype(jnp.bfloat16)
        dv_ref[src, 0, kc] += dot(p_scr[...], do_ref[0, qb], ((1,), (0,)))
        dk_ref[src, 0, kc] += dot(ds_scr[...], q_ref[0, qb], ((1,), (0,)))
        dqt_scr[qb] += dot(kt_scr[...], ds_scr[...], ((1,), (0,)))

    @pl.loop(0, num_src)
    def _(src):
        own = src == chip
        early = src < chip
        num_kc = jnp.where(early, num_chunks // 2, num_chunks)

        @pl.loop(0, num_kc)
        def _(kc):
            kt_scr[...] = k_ref[src, 0, kc].T

            @pl.when(own)
            def _():
                block(src, kc, kc, True)

            first = jnp.where(own, kc + 1, jnp.where(early, 0, num_chunks // 2))

            @pl.loop(first, num_chunks)
            def _(qb):
                block(src, kc, qb, False)

    for qb in range(num_chunks):
        for g in range(per_kv):
            dq_ref[0, qb, g] = dqt_scr[qb, :, g * chunk_len:(g + 1) * chunk_len].T * SM_SCALE


def attn_grads(q, d_out, stats, k_all, v_all):
    kv_heads, num_chunks, rows, _ = q.shape
    num_src, _, _, chunk_len, _ = k_all.shape
    per_kv = rows // chunk_len
    row_spec = pl.BlockSpec((1, num_chunks, rows, HEAD_DIM), lambda h: (h, 0, 0, 0))
    key_spec = pl.BlockSpec((num_src, 1, num_chunks, chunk_len, HEAD_DIM), lambda h: (0, h, 0, 0, 0))
    out_key = jax.ShapeDtypeStruct(k_all.shape, jnp.float32)
    return pl.pallas_call(
        functools.partial(attn_kernel, chunk_len, per_kv),
        grid=(kv_heads,),
        in_specs=[row_spec, row_spec,
                  pl.BlockSpec((1, num_chunks, 2, rows), lambda h: (h, 0, 0, 0)),
                  key_spec, key_spec],
        out_specs=[pl.BlockSpec((1, num_chunks, per_kv, chunk_len, HEAD_DIM), lambda h: (h, 0, 0, 0, 0)), key_spec, key_spec],
        out_shape=[jax.ShapeDtypeStruct((kv_heads, num_chunks, per_kv, chunk_len, HEAD_DIM), jnp.float32), out_key, out_key],
        scratch_shapes=[
            pltpu.VMEM((num_chunks, HEAD_DIM, rows), jnp.bfloat16),
            pltpu.VMEM((num_chunks, HEAD_DIM, rows), jnp.bfloat16),
            pltpu.VMEM((num_chunks, HEAD_DIM, rows), jnp.float32),
            pltpu.VMEM((HEAD_DIM, chunk_len), jnp.bfloat16),
            pltpu.VMEM((chunk_len, rows), jnp.bfloat16),
            pltpu.VMEM((chunk_len, rows), jnp.bfloat16),
        ],
        compiler_params=pltpu.CompilerParams(vmem_limit_bytes=56 * 2 ** 20),
        cost_estimate=pl.CostEstimate(flops=50_000_000_000, bytes_accessed=64_000_000, transcendentals=40_000_000),
        name='attn_grads',
    )(q, d_out, stats, k_all, v_all)


def solution(mesh):
    cp_size = mesh.shape['cp']
    num_chips = cp_size // CORES
    swap_pairs = [(dev, dev ^ 1) for dev in range(cp_size)]
    core_groups = [[chip * CORES + core for chip in range(num_chips)] for core in range(CORES)]

    def local_grads(q_raw, k_raw, v_proj, out_fwd, lse_fwd, d_out, q_norm, k_norm):
        dev_rank = lax.axis_index('cp')
        core, chip = dev_rank % CORES, dev_rank // CORES
        local_rows, num_heads = q_raw.shape[0], q_raw.shape[1]
        chunk_len = local_rows // 2
        kv_heads = k_raw.shape[1]
        per_kv = num_heads // kv_heads
        half = kv_heads // CORES

        def by_head(arr):
            n = arr.shape[1] // kv_heads
            arr = arr.reshape((2, chunk_len, CORES, half, n) + arr.shape[2:])
            return jnp.moveaxis(arr, (2, 3, 0, 4, 1), (0, 1, 2, 3, 4))

        def swap(arr):
            mine = lax.dynamic_index_in_dim(arr, core, 0, False)
            theirs = lax.ppermute(lax.dynamic_index_in_dim(arr, 1 - core, 0, False), 'cp', swap_pairs)
            first = jnp.where(core == 0, mine, theirs)
            second = jnp.where(core == 0, theirs, mine)
            return jnp.stack([first[:, 0], second[:, 0], second[:, 1], first[:, 1]], axis=1)

        def unswap(arr):
            first = jnp.stack([arr[:, 0], arr[:, 3]], axis=1)
            second = jnp.stack([arr[:, 1], arr[:, 2]], axis=1)
            mine = jnp.where(core == 0, first, second)
            theirs = lax.ppermute(jnp.where(core == 0, second, first), 'cp', swap_pairs)
            both = jnp.stack([jnp.where(core == 0, mine, theirs), jnp.where(core == 0, theirs, mine)])
            both = jnp.moveaxis(both, (2, 4, 0, 1, 3), (0, 1, 2, 3, 4))
            return both.reshape(local_rows, -1, HEAD_DIM)

        delta = jnp.sum(d_out.astype(jnp.float32) * out_fwd.astype(jnp.float32), axis=-1)
        stats = swap(by_head(jnp.stack([lse_fwd * LOG2E, delta], axis=-1)))
        stats = jnp.moveaxis(stats, -1, 2).reshape(half, 4, 2, per_kv * chunk_len)
        kv = swap(jnp.concatenate([by_head(k_raw), by_head(v_proj)], axis=3))
        q_x = swap(by_head(q_raw))
        do_x = swap(by_head(d_out)).reshape(half, 4, per_kv * chunk_len, HEAD_DIM)
        k_x, v_x = kv[:, :, 0], kv[:, :, 1]

        num_chunks = 2 * cp_size
        chunk_ids = jnp.stack([2 * chip, 2 * chip + 1, num_chunks - 2 - 2 * chip, num_chunks - 1 - 2 * chip])
        positions = chunk_ids[:, None] * chunk_len + jnp.arange(chunk_len)
        cos_t, sin_t = rope_tables(positions)
        q_full, pull_q = jax.vjp(lambda a, w: norm_rope(a, w, cos_t[None, :, None], sin_t[None, :, None]), q_x.astype(jnp.float32), q_norm)
        k_full, pull_k = jax.vjp(lambda a, w: norm_rope(a, w, cos_t[None], sin_t[None]), k_x.astype(jnp.float32), k_norm)
        q_b = q_full.astype(jnp.bfloat16).reshape(half, 4, per_kv * chunk_len, HEAD_DIM)
        k_b = k_full.astype(jnp.bfloat16)
        k_all = lax.all_gather(k_b, 'cp', axis_index_groups=core_groups)
        v_all = lax.all_gather(v_x, 'cp', axis_index_groups=core_groups)
        dq, dk_parts, dv_parts = attn_grads(q_b, do_x, stats, k_all, v_all)
        dk = lax.psum_scatter(dk_parts, 'cp', axis_index_groups=core_groups) * SM_SCALE
        dv = lax.psum_scatter(dv_parts, 'cp', axis_index_groups=core_groups)
        dq_raw, dq_weight = pull_q(dq)
        dk_raw, dk_weight = pull_k(dk)
        weights = lax.psum(jnp.stack([dq_weight, dk_weight]), 'cp')
        dkv = unswap(jnp.stack([dk_raw.astype(jnp.bfloat16), dv.astype(jnp.bfloat16)], axis=2))
        dkv = dkv.reshape(local_rows, kv_heads, 2, HEAD_DIM)
        return (unswap(dq_raw.astype(jnp.bfloat16)), dkv[:, :, 0], dkv[:, :, 1], weights[0], weights[1])

    row_spec = P(('dp', 'cp'))
    in_specs = (row_spec, row_spec, row_spec, row_spec, row_spec, row_spec, P(), P())
    out_specs = (row_spec, row_spec, row_spec, P('dp'), P('dp'))
    return jax.shard_map(local_grads, mesh=mesh, in_specs=in_specs, out_specs=out_specs, check_vma=False)
```

time: 1170 us -> 428 us (0.37)
  matrix products: 392 us -> 0 us
  waiting for transfers between devices: 461 us -> 158 us
  Pallas kernels: 0 us -> 120 us
  local copies, waits for them, and re-layouts: 113 us -> 30.5 us
  other arithmetic: 141 us -> 85.4 us
  starting transfers between devices: 27.5 us -> 5.45 us
  between operations: 1.47 us -> 14.4 us
    ppermute x30 -> x6, waiting for transfers between devices: 461 us -> 3.23 us  [the longest x4 3.23 us: swap(): lax.ppermute(lax.dynamic_index_in_dim(arr, 1 - core, 0, False), 'cp', swa...]
    dot_general x50 -> x0, matrix products: 392 us -> none  [the longest x10 90.7 us: pair_grads(): jnp.einsum('qngk,qngd->knd', prob_bf, do_blk, preferred_element_type=jnp....]
    pallas_call x0 -> x1, Pallas kernels: none -> 120 us  [attn_grads(): pl.pallas_call(functools.partial(attn_kernel, chunk_len, per_kv), grid=(k...]
    reduce_scatter x0 -> x2, waiting for transfers between devices: none -> 116 us  [the longest x1 72.5 us: local_grads(): dv = lax.psum_scatter(dv_parts, 'cp', axis_index_groups=core_groups)]
    concatenate x10 -> x1, other arithmetic: 58.4 us -> 0.73 us  [norm_rope(): jnp.concatenate([-normed[..., half_dim:], normed[..., :half_dim]], axis=-1)]
    while x20 -> x0, local copies, waits for them, and re-layouts: 45.2 us -> none  [the longest x6 31.6 us: local_grads(): lax.fori_loop(1, cp_size, visit_source, (k_b, v_proj, dq_acc, dk_acc, dv_...]
    slice x28 -> x6, local copies, waits for them, and re-layouts: 46.8 us -> 1.77 us  [the longest x1 1.15 us: local_grads(): k_x, v_x = (kv[:, :, 0], kv[:, :, 1])]
    all_gather x0 -> x2, waiting for transfers between devices: none -> 38.4 us  [the longest x1 38.4 us: local_grads(): k_all = lax.all_gather(k_b, 'cp', axis_index_groups=core_groups)]
  transfers between devices with their start and end apart: 30 -> 10, of which waited for: 14 -> 5; matrix products, arithmetic and copies ran while one was open for 6% -> 23% of each run, Pallas kernels for 0% -> 0%
where the time goes in v1:
time: 428 us; the launch traced here: 427 us
  waiting for transfers between devices  158 us (37%)
  Pallas kernels  120 us (28%)
  other arithmetic  85.4 us (20%)
  local copies, waits for them, and re-layouts  30.5 us (7%)
  between operations  14.4 us (3%)
  blocking collectives  12.7 us (3%)
  starting transfers between devices  5.45 us (1%)
    pallas_call x1, Pallas kernels, attn_grads(): pl.pallas_call(functools.partial(attn_kernel, chunk_len, per_kv), grid=(k...  120 us
    reduce_scatter x1, waiting for transfers between devices, local_grads(): dv = lax.psum_scatter(dv_parts, 'cp', axis_index_groups=core_groups)  72.5 us
    reduce_scatter x1, waiting for transfers between devices, local_grads(): lax.psum_scatter(dk_parts, 'cp', axis_index_groups=core_groups) * SM_SCALE  43.2 us
    all_gather x1, waiting for transfers between devices, local_grads(): k_all = lax.all_gather(k_b, 'cp', axis_index_groups=core_groups)  38.4 us
    unnamed x60, local copies, waits for them, and re-layouts  17.4 us
    reduce_sum x2, other arithmetic, norm_rope(): normed = raw_in * lax.rsqrt(mean_sq + NORM_EPS) * weight  14.2 us
    psum x1, blocking collectives, local_grads(): weights = lax.psum(jnp.stack([dq_weight, dk_weight]), 'cp')  12.7 us
    convert_element_type x1, other arithmetic, local_grads(): q_full.astype(jnp.bfloat16).reshape(half, 4, per_kv * chunk_len, HEAD_DIM)  9.71 us
  transfers between devices with their start and end apart: 10, of which 5 were waited for; matrix products, arithmetic and copies ran while one was open for 23% of the time, Pallas kernels for 0%

profile of v1, /device:TPU:81, one launch (start us, length us, event | category | flops | bytes accessed | tf_op | source)
XLA Modules:
  0.0 427.1 jit_solution(5269013071235429280)
XLA Ops:
  7.3 2.0 copy_bitcast_fusion.4
  9.4 2.1 collective-permute-start.3
  11.5 2.3 collective-permute-done.3
  16.8 6.4 %constant_dynamic-slice_fusion.1 = (bf16[2,256,1,4,4,128]{5,4,3,2,1,0:T(4,128)(2,1)}, bf16[2,256,1,4,4,128]{5,4,3,2,1,0:T(4,128)(2,1)S(1)}, bf16[2,256,1,4,4,128...) fusion(bf16[2,256,2,4,4,128]{5,4,3,2,1,0:T(4,128)(2,1)} %bitcast.160, s32[]{:T(128)S(6)} %select_n.104, ...), kind=kLoop, calls=%fused_computation.116 | loop fusion | bytes 16777224 | tf_op jit(solution)/shard_map/dynamic-slice.2
  23.2 1.9 copy.72
  25.4 1.9 copy.71
  27.9 2.9 broadcast_multiply_fusion.2
  32.9 2.0 fusion.21
  35.4 5.7 %multiply_reduce_fusion = f32[512,32]{1,0:T(8,128)S(1)} fusion(bf16[512,32,128]{2,1,0:T(8,128)(2,1)} %param.11, bf16[512,32,128]{2,1,0:T(8,128)(2,1)} %param.13), kind=kLoop, calls=%fused_computation.17 | loop fusion | flops 8372224 | bytes 8454144 | tf_op jit(solution)/shard_map/reduce_sum | solution.py:157
  43.7 2.8 broadcast_select_fusion.4
  46.7 2.4 fusion.4
  49.2 2.8 broadcast_select_fusion.2
  52.2 2.3 pad_maximum_fusion.1
  54.5 2.4 fusion.1
  56.9 5.1 %slice_negate_fusion.1 = (f32[4,4,4,256,64]{4,3,2,1,0:T(8,128)S(1)}, f32[4,4,4,256,64]{4,3,2,1,0:T(8,128)}) fusion(f32[4,4,4,256,128]{4,3,2,1,0:T(8,128)S(1)} %fusion.1), kind=kLoop, calls=%fused_computation.12 | loop fusion | flops 1048576 | bytes 16777216 | tf_op jit(solution)/shard_map/jvp()/neg | solution.py:29
  63.4 9.7 %fusion.7.q_ref = bf16[4,4,1024,128]{3,2,1,0:T(8,128)(2,1)} fusion(f32[4,4,1024,64]{3,2,1,0:T(8,128)} %bitcast.158, f32[4,4,1024,64]{3,2,1,0:T(8,128)S(1)} %bitcast.157, bf16[4,1,1024,128]{3,2,1,0:T(8,128)(2,1)S(1)} %bitcast.154, bf16[4,2,1024,128]{3,2,1,0:T(8,128)(2,1)S(1)} %bitcast.152, bf16[4,1,1024,128]{3,2,1,0:T(8,128)(2,1)S(1)} %bitcast.153, ...), kind=kLoop, calls=%fused_computation.15 | loop fusion | flops 20971520 | bytes 21037568 | tf_op jit(solution)/shard_map/convert_element_type | solution.py:171
  73.1 38.4 %all-gather.4.cloned.1.call-done.k_ref = bf16[4,4,4,256,128]{4,3,2,1,0:T(8,128)(2,1)} async-done(((bf16[1,4,4,256,128]{4,3,2,1,0:T(8,128)(2,1)}), bf16[4,4,4,256,128]{4,3,2,1,0:T(8,128)(2,1)}) %all-gather.4.cloned.1.call-update) | async-done | bytes 4194320 | tf_op jit(solution)/shard_map/all_gather | solution.py:173
  111.5 120.5 %attn_grads.1 = (f32[4,4,4,256,128]{4,3,2,1,0:T(8,128)}, f32[4,4,4,256,128]{4,3,2,1,0:T(8,128)}, f32[4,4,4,256,128]{4,3,2,1,0:T(8,128)}) custom-call(bf16[4,4,1024,128]{3,2,1,0:T(8,128)(2,1)} %fusion.7.q_ref, bf16[4,4,1024,128]{3,2,1,0:T(8,128)(2,1)} %bitcast.164, f32[4,4,2,1024]{3,2,1,0:T(2,128)} %reshape.273.st_ref, ...), custom_call_target="tpu_custom_call" | custom-call | flops 49999998976 | bytes 64000000 | tf_op jit(solution)/shard_map/attn_grads/pallas_call | solution.py:99
  232.7 4.3 broadcast_multiply_fusion
  237.0 7.5 %fusion.43 = (f32[4,4,4,256,64]{4,3,2,1,0:T(8,128)}, f32[4,4,4,256,64]{4,3,2,1,0:T(8,128)}) fusion(f32[4,4,4,256,128]{4,3,2,1,0:T(8,128)S(1)} %broadcast_multiply_fusion), kind=kLoop, calls=%fused_computation.124 | loop fusion | flops 1048576 | bytes 16777216 | tf_op jit(solution)/shard_map/transpose(jvp())/split | solution.py:29
  244.6 11.3 %fusion.2 = (f32[128]{0:T(128)S(1)}, f32[4,4,4,256]{3,2,1,0:T(4,128)S(1)}, f32[4,4,4,256,128]{4,3,2,1,0:T(8,128)S(1)}) fusion(f32[4,4,4,256]{3,2,1,0:T(4,128)S(1)} %fusion.40, bf16[4,1,4,256,128]{4,3,2,1,0:T(8,128)(2,1)S(1)} %copy-done.2, bf16[4,2,4,256,128]{4,3,2,1,0:T(8,128)(2,1)S(1)} %get-tuple-element.39, ...), kind=kLoop, calls=%fused_computation.7 | loop fusion | flops 25149312 | bytes 30016512 | tf_op jit(solution)/shard_map/transpose(jvp())/reduce_sum | solution.py:27
  256.0 5.0 %fusion.3 = bf16[4,4,4,256,128]{4,3,2,1,0:T(8,128)(2,1)S(1)} fusion(f32[4,4,4,256,128]{4,3,2,1,0:T(8,128)S(1)} %get-tuple-element.26, f32[4,4,4,256]{3,2,1,0:T(4,128)S(1)} %multiply_multiply_fusion, f32[128]{0:T(128)S(1)} %copy-done.24, f32[4,4,4,256]{3,2,1,0:T(4,128)S(1)} %fusion.40, bf16[4,1,4,256,128]{4,3,2,1,0:T(8,128)(2,1)S(1)} %copy-done.2, ...), kind=kLoop, calls=%fused_computation.8 | loop fusion | flops 18874368 | bytes 16908800 | tf_op jit(solution)/shard_map/convert_element_type | solution.py:183
  261.3 1.8 copy-done.5
  265.6 43.2 %reduce-scatter.3.cloned.1.call-done = f32[1,4,4,256,128]{4,3,2,1,0:T(8,128)} async-done(((f32[4,4,4,256,128]{4,3,2,1,0:T(8,128)}), f32[1,4,4,256,128]{4,3,2,1,0:T(8,128)}) %reduce-scatter.3.cloned.1.call-update) | async-done | bytes 2097168 | tf_op jit(solution)/shard_map/reduce_scatter | solution.py:176
  308.9 1.7 bitcast_multiply_fusion
  312.9 2.8 fusion.14
  315.8 72.5 %reduce-scatter.5.cloned.1.call-done = f32[1,4,4,256,128]{4,3,2,1,0:T(8,128)} async-done(((f32[4,4,4,256,128]{4,3,2,1,0:T(8,128)}), f32[1,4,4,256,128]{4,3,2,1,0:T(8,128)}) %reduce-scatter.5.cloned.1.call-update) | async-done | bytes 2097168 | tf_op jit(solution)/shard_map/reduce_scatter | solution.py:177
  388.3 1.9 convert_bitcast_fusion.2
  394.2 1.8 select_bitcast_fusion.1
  396.9 4.7 %copy.45 = bf16[512,32,128]{2,1,0:T(8,128)(2,1)} copy(bf16[512,32,128]{2,0,1:T(8,128)(2,1)S(1)} %bitcast.159) | data formatting | bytes 8388608
  401.6 12.7 %psum.7 = f32[2,128]{1,0:T(2,128)S(1)} all-reduce(f32[2,128]{1,0:T(2,128)S(1)} %pad_maximum_fusion.6), channel_id=1, replica_groups=mesh['dp'=4,'cp'=8] {'cp'}, use_global_device_ids=true, to_apply=%region_9.10 | all-reduce | flops 256 | bytes 2048 | tf_op jit(solution)/shard_map/psum | solution.py:180
  414.9 1.8 select_bitcast_fusion.3
  (120 shorter events, 25.7 us)
Async XLA Ops:
  7.2 65.9 %all-gather.6.cloned.1.call-start = ((), (), s32[]{:S(2)}) async-start(), calls=%async_computation.5 | async-start | bytes 5242880 | tf_op jit(solution)/shard_map/all_gather | solution.py:174
  9.4 4.4 %collective-permute-start.3 = (bf16[4,2,2,256,128]{4,3,1,0,2:T(8,128)(2,1)S(1)}, bf16[4,2,2,256,128]{4,3,1,0,2:T(8,128)(2,1)}, u32[]{:S(2)}, u32[]{:S(2)}) collective-permute-start(bf16[4,2,2,256,128]{4,3,1,0,2:T(8,128)(2,1)S(1)} %fusion.35), channel_id=1, source_target_pairs={{0,1},{1,0},{2,3},{3,2},{4,5},{5,4},{6,7},{7,6},{8,9},{9,8},{10,11... | collective-permute-start | bytes 3145736 | tf_op jit(solution)/shard_map/ppermute | solution.py:143
  15.5 17.4 %copy-start.3 = (bf16[4,4,2,256,128]{4,3,1,0,2:T(8,128)(2,1)}, bf16[4,4,2,256,128]{4,3,1,0,2:T(8,128)(2,1)S(1)}, u32[]{:S(2)}) copy-start(bf16[4,4,2,256,128]{4,3,1,0,2:T(8,128)(2,1)S(1)} %pad_maximum_fusion.2) | copy-start | bytes 6291460
  16.7 94.8 %all-gather.4.cloned.1.call-start = ((), (), s32[]{:S(2)}) async-start(), calls=%async_computation.2 | async-start | bytes 5242880 | tf_op jit(solution)/shard_map/all_gather | solution.py:173
  25.1 18.6 %collective-permute-start = (bf16[4,2,4,256,128]{4,3,2,1,0:T(8,128)(2,1)}, bf16[4,2,4,256,128]{4,3,2,1,0:T(8,128)(2,1)}, u32[]{:S(2)}, u32[]{:S(2)}) collective-permute-start(bf16[4,2,4,256,128]{4,3,2,1,0:T(8,128)(2,1)} %bitcast.151), channel_id=1, source_target_pairs={{0,1},{1,0},{2,3},{3,2},{4,5},{5,4},{6,7},{7,6},{8,9},{9,8},{10,11... | collective-permute-start | bytes 6291464 | tf_op jit(solution)/shard_map/ppermute | solution.py:143
  27.3 21.8 %collective-permute-start.1 = (bf16[4,2,4,256,128]{4,3,2,1,0:T(8,128)(2,1)}, bf16[4,2,4,256,128]{4,3,2,1,0:T(8,128)(2,1)}, u32[]{:S(2)}, u32[]{:S(2)}) collective-permute-start(bf16[4,2,4,256,128]{4,3,2,1,0:T(8,128)(2,1)} %bitcast.150), channel_id=1, source_target_pairs={{0,1},{1,0},{2,3},{3,2},{4,5},{5,4},{6,7},{7,6},{8,9},{9,8},{10,11... | collective-permute-start | bytes 6291464 | tf_op jit(solution)/shard_map/ppermute | solution.py:143
  27.7 3.8 copy-start.23
  30.8 2.1 copy-start.13
  30.8 2.1 copy-start.18
  32.9 2.4 copy-start.22
  35.1 273.8 %reduce-scatter.3.cloned.1.call-start = ((), (), s32[]{:S(2)}) async-start(), calls=%async_computation.3 | async-start | bytes 10485760 | tf_op jit(solution)/shard_map/reduce_scatter | solution.py:176
  41.3 1.4 collective-permute-start.2
  46.7 2.4 copy-start
  52.1 2.3 copy-start.1
  52.2 2.3 copy-start.24
  56.9 5.2 %copy-start.19 = (f32[4,256,128]{2,1,0:T(8,128)S(1)}, f32[4,256,128]{2,1,0:T(8,128)}, u32[]{:S(2)}) copy-start(f32[4,256,128]{2,1,0:T(8,128)} %copy-done.18) | copy-start | bytes 1572868
  232.1 156.2 %reduce-scatter.5.cloned.1.call-start = ((), (), s32[]{:S(2)}) async-start(), calls=%async_computation.4 | async-start | bytes 10485760 | tf_op jit(solution)/shard_map/reduce_scatter | solution.py:177
  232.7 11.9 %slice-start = ((s8[8388608]{0:T(1024)(128)(4,1)}), s8[4194304]{0:T(1024)(128)(4,1)S(1)}, s32[]{:S(2)}) async-start(s8[8388608]{0:T(1024)(128)(4,1)} %bitcast.155), calls=%async_computation.6 | async-start | bytes 8388608
  237.0 7.6 %copy-start.2 = (bf16[4,1,4,256,128]{4,3,2,1,0:T(8,128)(2,1)S(1)}, bf16[4,1,4,256,128]{4,3,2,1,0:T(8,128)(2,1)}, u32[]{:S(2)}) copy-start(bf16[4,1,4,256,128]{4,3,2,1,0:T(8,128)(2,1)} %copy-done) | copy-start | bytes 3145732
  237.0 7.6 %slice-start.1 = ((s8[8388608]{0:T(1024)(128)(4,1)}), s8[4194304]{0:T(1024)(128)(4,1)S(1)}, s32[]{:S(2)}) async-start(s8[8388608]{0:T(1024)(128)(4,1)} %bitcast.155), calls=%async_computation.7 | async-start | bytes 8388608
  237.0 7.6 %copy-start.15 = (f32[4,256,128]{2,1,0:T(8,128)S(1)}, f32[4,256,128]{2,1,0:T(8,128)}, u32[]{:S(2)}) copy-start(f32[4,256,128]{2,1,0:T(8,128)} %copy-done.13) | copy-start | bytes 1572868
  261.0 2.0 copy-start.5
  261.3 3.4 copy-start.9
  261.3 3.4 copy-start.11
  263.1 45.8 %copy-start.21 = (f32[4,256,128]{2,1,0:T(8,128)S(1)}, f32[4,256,128]{2,1,0:T(8,128)}, u32[]{:S(2)}) copy-start(f32[4,256,128]{2,1,0:T(8,128)} %get-tuple-element.60) | copy-start | bytes 1572868
  264.7 129.4 %collective-permute-start.4 = (bf16[4,2,4,256,128]{4,3,2,1,0:T(8,128)(2,1)}, bf16[4,2,4,256,128]{4,3,2,1,0:T(8,128)(2,1)}, u32[]{:S(2)}, u32[]{:S(2)}) collective-permute-start(bf16[4,2,4,256,128]{4,3,2,1,0:T(8,128)(2,1)} %broadcast_select_fusion), channel_id=1, source_target_pairs={{0,1},{1,0},{2,3},{3,2},{4,5},{5,4},{6,7},{7,6},{8,9},{9,8},{10,11... | collective-permute-start | bytes 6291464 | tf_op jit(solution)/shard_map/ppermute | solution.py:152
  310.6 2.2 copy-start.16
  310.6 2.3 copy-start.20
  388.3 2.2 copy-start.17
  390.5 3.6 copy-start.6
  393.0 21.9 %collective-permute-start.5 = (bf16[4,2,2,256,128]{4,3,1,0,2:T(8,128)(2,1)S(1)}, bf16[4,2,2,256,128]{4,3,1,0,2:T(8,128)(2,1)}, u32[]{:S(2)}, u32[]{:S(2)}) collective-permute-start(bf16[4,2,2,256,128]{4,3,1,0,2:T(8,128)(2,1)S(1)} %broadcast_select_fusion.6), channel_id=1, source_target_pairs={{0,1},{1,0},{2,3},{3,2},{4,5},{5,4},{6,7},{7,6},{8,9},{9,8},{10,11... | collective-permute-start | bytes 3145736 | tf_op jit(solution)/shard_map/ppermute | solution.py:152
  396.9 18.0 %copy-start.8 = (bf16[4,4,1,256,128]{4,3,1,0,2:T(8,128)(2,1)S(1)}, bf16[4,4,1,256,128]{4,3,1,0,2:T(8,128)(2,1)}, u32[]{:S(2)}) copy-start(bf16[4,4,1,256,128]{4,3,1,0,2:T(8,128)(2,1)} %copy-done.7) | copy-start | bytes 3145732
  (5 other events, 6.5 us)
Sparse Core Ops, SparseCore 0:
  16.8 47.1 all-gather.5
  66.1 45.3 all-gather.3
  232.2 76.6 reduce-scatter.2
  311.1 77.1 reduce-scatter.4

commit v2 on v0

v2 whole, which is shorter than its diff:
```python
import functools

import jax
import jax.numpy as jnp
from jax import lax
from jax.experimental import pallas as pl
from jax.experimental.pallas import tpu as pltpu
from jax.sharding import PartitionSpec as P

HEAD_DIM = 128
ROPE_THETA = 1000000.0
NORM_EPS = 1e-6
LOG2E = 1.4426950408889634
SM_SCALE = HEAD_DIM ** -0.5
CORES = 2
MESH = pl.DeviceIdType.MESH


def rope_tables(positions):
    inv_freq = ROPE_THETA ** (-jnp.arange(0, HEAD_DIM, 2).astype(jnp.float32) / HEAD_DIM)
    angles = positions.astype(jnp.float32)[..., None] * inv_freq
    cos_t, sin_t = jnp.cos(angles), jnp.sin(angles)
    return jnp.concatenate([cos_t, cos_t], axis=-1), jnp.concatenate([-sin_t, sin_t], axis=-1)


def swap_halves(arr):
    return pltpu.roll(arr, HEAD_DIM // 2, arr.ndim - 1)


def inverse_rms(raw_in):
    return lax.rsqrt(jnp.mean(raw_in * raw_in, axis=-1, keepdims=True) + NORM_EPS)


def norm_rope_pull(raw_in, weight, cos_t, sin_t, grad):
    inv_rms = inverse_rms(raw_in)
    unit = raw_in * inv_rms
    grad_normed = grad * cos_t - swap_halves(grad) * sin_t
    weight_terms = grad_normed * unit
    grad_unit = grad_normed * weight
    grad_raw = inv_rms * (grad_unit - unit * jnp.mean(grad_unit * unit, axis=-1, keepdims=True))
    return grad_raw, weight_terms.reshape(-1, 8, HEAD_DIM).sum(0)


def dot(a, b):
    return lax.dot_general(a, b, (((1,), (0,)), ((), ())), preferred_element_type=jnp.float32)


def attn_kernel(num_chips, q_hbm, do_hbm, st_hbm, kv_hbm, k_raw, cos_q, sin_q, cos_k, sin_k, wq, wk,
                dq_hbm, dk_out, dv_out, dw_out,
                q_buf, do_buf, st_buf, kv_buf, q_now, qt_now, dot_now, dqt_now, kt_now, p_now, ds_now,
                acc, own_acc, own_recv, send_buf, transit, part, total, dw_acc, dw_all,
                ex_send, ex_recv, ex_local, own_send, own_kv_recv, own_local, nb_send, nb_recv, rl_send, op_recv,
                pt_send, pt_recv, tr_send, tr_recv, fw_send, fw_recv, oa_send, oa_recv,
                dq_send, dq_recv, dq_local, dw_send, dw_recv):
    me = lax.axis_index('cp')
    chip, core = me // CORES, me % CORES
    left, right = (chip + num_chips - 1) % num_chips, (chip + 1) % num_chips
    far = (chip + 2) % num_chips
    heads = q_buf.shape[0]
    num_chunks, chunk_len = kv_buf.shape[2], kv_buf.shape[4]
    per_kv = q_buf.shape[2] // chunk_len

    def remote(src, dst, send_sem, recv_sem, to_chip, to_core):
        return pltpu.make_async_remote_copy(src_ref=src, dst_ref=dst, send_sem=send_sem, recv_sem=recv_sem,
                                            device_id={'cp': to_chip * CORES + to_core}, device_id_type=MESH)

    def place(of_core, ch):
        return of_core if ch == 0 else num_chunks - 1 - of_core

    exchanged = ((q_hbm, q_buf), (do_hbm, do_buf), (st_hbm, st_buf))

    def ex_copies(h):
        for a, (src, dst) in enumerate(exchanged):
            for ch in range(2):
                mine = place(core, ch)
                yield (remote(src.at[(1 - core) * heads + h, ch], dst.at[h, mine], ex_send.at[h, a, ch], ex_recv.at[h, a, ch], chip, 1 - core),
                       remote(src.at[(1 - core) * heads + h, ch], dst.at[h, place(1 - core, ch)], ex_send.at[h, a, ch], ex_recv.at[h, a, ch], chip, 1 - core),
                       pltpu.make_async_copy(src.at[core * heads + h, ch], dst.at[h, mine], ex_local.at[h, a, ch]))

    def own_copies(h):
        for ch in range(2):
            mine = place(core, ch)
            yield (remote(kv_hbm.at[(1 - core) * heads + h, ch], kv_buf.at[0, h, mine], own_send.at[h, ch], own_kv_recv.at[h, ch], chip, 1 - core),
                   remote(kv_hbm.at[(1 - core) * heads + h, ch], kv_buf.at[0, h, place(1 - core, ch)], own_send.at[h, ch], own_kv_recv.at[h, ch], chip, 1 - core),
                   pltpu.make_async_copy(kv_hbm.at[core * heads + h, ch], kv_buf.at[0, h, mine], own_local.at[h, ch]))

    def nb_out(h, to_core, ch, way):
        return remote(kv_hbm.at[to_core * heads + h, ch], kv_buf.at[3 if way == 0 else 1, h, place(core, ch)],
                      nb_send.at[h, to_core, ch, way], nb_recv.at[h, place(core, ch), way], right if way == 0 else left, to_core)

    def second_sent(way):
        return chip >= 2 if way == 0 else chip >= 1

    def nb_each(h, fn):
        for way in range(2):
            for to_core in range(CORES):
                fn(nb_out(h, to_core, 0, way))

            @pl.when(second_sent(way))
            def _():
                for to_core in range(CORES):
                    fn(nb_out(h, to_core, 1, way))

    def nb_wait(h, way):
        slot = 3 if way == 0 else 1

        def wait(idx):
            remote(kv_hbm.at[0, 0], kv_buf.at[slot, h, idx], nb_send.at[h, 0, 0, way], nb_recv.at[h, idx, way], left, core).wait_recv()

        wait(0)
        wait(1)

        @pl.when(left >= 2 if way == 0 else right >= 1)
        def _():
            wait(2)
            wait(3)

    def relay(h, second, kind):
        src_slot, to_chip = (3, right) if kind == 0 else (1, left)
        pair = pl.ds(2 * second, 2)
        return remote(kv_buf.at[src_slot, h, pair, kind], kv_buf.at[2, h, pair, kind], rl_send.at[h, second, kind], op_recv.at[h, second, kind], to_chip, core)

    def relay_each(h, fn):
        for kind in range(2):
            fn(relay(h, 0, kind))

            @pl.when(right < left if kind == 0 else left < right)
            def _():
                fn(relay(h, 1, kind))

    def part_out(h, off, idx):
        to_chip = right if off == 1 else left
        home_core = idx if idx < 2 else num_chunks - 1 - idx
        return remote(send_buf.at[h, off - 1, idx], part.at[2 if off == 1 else 0, core * heads + h, idx // 2],
                      pt_send.at[h, off // 2, idx], pt_recv.at[1 if off == 1 else 0, core * heads + h, idx // 2], to_chip, home_core)

    def transit_out(h, second, kind):
        pair = pl.ds(2 * second, 2)
        return remote(send_buf.at[h, 1, pair, kind], transit.at[h, kind, pair], tr_send.at[h, second, kind], tr_recv.at[h, second, kind],
                      right if kind == 0 else left, core)

    def forward_out(h, idx, kind):
        home_core = idx if idx < 2 else num_chunks - 1 - idx
        return remote(transit.at[h, kind, idx], part.at[1, core * heads + h, idx // 2, kind],
                      fw_send.at[h, idx, kind], fw_recv.at[core * heads + h, idx // 2, kind], right if kind == 0 else left, home_core)

    def forward_each(h, fn):
        for kind in range(2):
            fn(h, 0, kind)

            @pl.when(left < right if kind == 0 else right < left)
            def _():
                fn(h, 1, kind)

    def start_forward(h, second, kind):
        transit_out(h, second, kind).wait_recv()
        for idx in (2 * second, 2 * second + 1):
            forward_out(h, idx, kind).start()

    def end_forward(h, second, kind):
        for idx in (2 * second, 2 * second + 1):
            forward_out(h, idx, kind).wait_send()

    def own_out(h, ch):
        return remote(own_acc.at[h, place(1 - core, ch)], own_recv.at[h, ch], oa_send.at[h, ch], oa_recv.at[h, ch], chip, 1 - core)

    def dq_copies(h):
        for ch in range(2):
            yield (remote(q_buf.at[h, place(1 - core, ch)], dq_hbm.at[core * heads + h, ch], dq_send.at[h, ch], dq_recv.at[h, ch], chip, 1 - core),
                   remote(q_buf.at[h, place(1 - core, ch)], dq_hbm.at[(1 - core) * heads + h, ch], dq_send.at[h, ch], dq_recv.at[h, ch], chip, 1 - core),
                   pltpu.make_async_copy(q_buf.at[h, place(core, ch)], dq_hbm.at[core * heads + h, ch], dq_local.at[h, ch]))

    def dw_out_to(step):
        peer = (me + step) % (num_chips * CORES)
        return remote(dw_acc, dw_all.at[me], dw_send.at[step], dw_recv.at[me], peer // CORES, peer % CORES)

    def block(h, off, kc, qb, masked):
        k_blk, v_blk = kv_buf[off, h, kc, 0], kv_buf[off, h, kc, 1]
        if masked:
            key_pos = lax.broadcasted_iota(jnp.int32, (chunk_len, chunk_len), 0)
            query_pos = lax.broadcasted_iota(jnp.int32, (chunk_len, chunk_len), 1)
            visible = key_pos <= query_pos
        for g in range(per_kv):
            cols = pl.ds(g * chunk_len, chunk_len)
            logits = dot(k_blk, qt_now[qb, :, cols]) * (SM_SCALE * LOG2E) - st_buf[h, qb, 0, g:g + 1, :]
            if masked:
                logits = jnp.where(visible, logits, -jnp.inf)
            prob = jnp.exp2(logits)
            dprob = dot(v_blk, dot_now[qb, :, cols])
            p_now[:, cols] = prob.astype(jnp.bfloat16)
            ds_now[:, cols] = (prob * (dprob - st_buf[h, qb, 1, g:g + 1, :])).astype(jnp.bfloat16)
        acc[kc, 1] += dot(p_now[...], do_buf[h, qb])
        acc[kc, 0] += dot(ds_now[...], q_now[qb])
        dqt_now[qb] += dot(kt_now[...], ds_now[...])

    def source_block(h, off):
        src = (chip + off) % num_chips
        own = off == 0
        early = src < chip
        acc[...] = jnp.zeros_like(acc)

        @pl.loop(0, jnp.where(early, num_chunks // 2, num_chunks))
        def _(kc):
            kt_now[...] = kv_buf[off, h, kc, 0].T

            @pl.when(own)
            def _():
                block(h, off, kc, kc, True)

            @pl.loop(jnp.where(own, kc + 1, jnp.where(early, 0, num_chunks // 2)), num_chunks)
            def _(qb):
                block(h, off, kc, qb, False)

    barrier = pltpu.get_barrier_semaphore()
    for step in range(1, num_chips * CORES):
        pl.semaphore_signal(barrier, inc=1, device_id={'cp': (me + step) % (num_chips * CORES)}, device_id_type=MESH)
    pl.semaphore_wait(barrier, num_chips * CORES - 1)

    nb_each(0, lambda copy: copy.start())

    @pl.loop(0, heads)
    def _(h):
        for out, _, local in own_copies(h):
            out.start()
            local.start()
        for out, _, local in ex_copies(h):
            out.start()
            local.start()

    dw_acc[...] = jnp.zeros_like(dw_acc)

    @pl.loop(0, heads)
    def _(h):
        for copies in (own_copies(h), ex_copies(h)):
            for out, arriving, local in copies:
                out.wait_send()
                arriving.wait_recv()
                local.wait()
        dqt_now[...] = jnp.zeros_like(dqt_now)

        @pl.loop(0, num_chunks)
        def _(qb):
            for g in range(per_kv):
                rows = pl.ds(g * chunk_len, chunk_len)
                raw = q_buf[h, qb, rows, :].astype(jnp.float32)
                normed = raw * inverse_rms(raw) * wq[...]
                query = (normed * cos_q[qb] + swap_halves(normed) * sin_q[qb]).astype(jnp.bfloat16)
                q_now[qb, rows, :] = query
                qt_now[qb, :, rows] = query.T
            dot_now[qb] = do_buf[h, qb].T

        last = h == heads - 1

        @pl.loop(0, num_chips)
        def _(j):
            first_order = jnp.where(j == 0, 0, jnp.where(j == 1, 1, jnp.where(j == 2, 3, 2)))
            last_order = jnp.where(j == 0, 2, jnp.where(j == 1, 1, jnp.where(j == 2, 3, 0)))
            off = jnp.where(last, last_order, first_order)

            @pl.when(off == 2)
            def _():
                for kind in range(2):
                    relay(h, 0, kind).wait_recv()

                @pl.when(chip < far)
                def _():
                    for kind in range(2):
                        relay(h, 1, kind).wait_recv()

            source_block(h, off)
            src = (chip + off) % num_chips

            @pl.when(off == 0)
            def _():
                own_acc[h] = acc[...]
                for ch in range(2):
                    own_out(h, ch).start()

            @pl.when(off != 0)
            def _():
                send_buf[h, off - 1, 0:2] = acc[0:2].astype(jnp.bfloat16)

                @pl.when(chip < src)
                def _():
                    send_buf[h, off - 1, 2:4] = acc[2:4].astype(jnp.bfloat16)

            for side in (1, 3):
                @pl.when(off == side)
                def _():
                    part_out(h, side, 0).start()
                    part_out(h, side, 1).start()

                    @pl.when(chip < src)
                    def _():
                        part_out(h, side, 2).start()
                        part_out(h, side, 3).start()

            @pl.when(off == 2)
            def _():
                for kind in range(2):
                    transit_out(h, 0, kind).start()

                @pl.when(chip < src)
                def _():
                    for kind in range(2):
                        transit_out(h, 1, kind).start()

            def pass_keys(of_head):
                nb_wait(of_head, 0)
                nb_wait(of_head, 1)
                relay_each(of_head, lambda copy: copy.start())

                @pl.when(of_head + 1 < heads)
                def _():
                    nb_each(of_head + 1, lambda copy: copy.start())

            @pl.when((h == 0) & (j == 0))
            def _():
                pass_keys(0)

            @pl.when((j == 2) & (h + 1 < heads))
            def _():
                pass_keys(h + 1)

            @pl.when((j == 0) & (h > 0))
            def _():
                forward_each(h - 1, start_forward)

            @pl.when((j == 2) & last)
            def _():
                forward_each(h, start_forward)

        @pl.loop(0, num_chunks)
        def _(qb):
            for g in range(per_kv):
                rows = pl.ds(g * chunk_len, chunk_len)
                grad = dqt_now[qb, :, rows].T * SM_SCALE
                raw = q_buf[h, qb, rows, :].astype(jnp.float32)
                grad_raw, terms = norm_rope_pull(raw, wq[...], cos_q[qb], sin_q[qb], grad)
                q_buf[h, qb, rows, :] = grad_raw.astype(jnp.bfloat16)
                dw_acc[0] += terms

        for out, _, local in dq_copies(h):
            out.start()
            local.start()

    def home(head, h, own):
        for ch in range(2):
            mine = place(core, ch)
            total[...] = own_acc[h, mine] if own else own_recv[h, ch]

            def add(slot):
                total[...] += part[slot, head, ch].astype(jnp.float32)

            def take_side(way):
                remote(send_buf.at[0, 0, 0], part.at[2 * way, head, ch], pt_send.at[0, 0, 0], pt_recv.at[way, head, ch], left, core).wait_recv()
                add(2 * way)

            def take_far():
                for kind in range(2):
                    remote(transit.at[0, 0, 0], part.at[1, head, ch, kind], fw_send.at[0, 0, 0], fw_recv.at[head, ch, kind], left, core).wait_recv()
                add(1)

            if ch == 0:
                take_side(0)
                take_side(1)
                take_far()
            else:
                @pl.when(right < chip)
                def _():
                    take_side(0)

                @pl.when(left < chip)
                def _():
                    take_side(1)

                @pl.when(far < chip)
                def _():
                    take_far()

            raw = k_raw[head, ch].astype(jnp.float32)
            grad_raw, terms = norm_rope_pull(raw, wk[...], cos_k[ch], sin_k[ch], total[0] * SM_SCALE)
            dk_out[head, ch] = grad_raw.astype(jnp.bfloat16)
            dv_out[head, ch] = total[1].astype(jnp.bfloat16)
            dw_acc[1] += terms

    @pl.loop(0, heads)
    def _(h):
        for ch in range(2):
            own_out(h, ch).wait_recv()
            own_out(h, ch).wait_send()
        home((1 - core) * heads + h, h, False)
        home(core * heads + h, h, True)

    for step in range(1, num_chips * CORES):
        dw_out_to(step).start()
    dw_all[me] = dw_acc[...]

    @pl.loop(0, heads)
    def _(h):
        nb_each(h, lambda copy: copy.wait_send())
        relay_each(h, lambda copy: copy.wait_send())
        for off in (1, 3):
            part_out(h, off, 0).wait_send()
            part_out(h, off, 1).wait_send()

            @pl.when(chip < (chip + off) % num_chips)
            def _():
                part_out(h, off, 2).wait_send()
                part_out(h, off, 3).wait_send()
        for kind in range(2):
            transit_out(h, 0, kind).wait_send()

        @pl.when(chip < far)
        def _():
            for kind in range(2):
                transit_out(h, 1, kind).wait_send()
        forward_each(h, end_forward)
        for out, arriving, local in dq_copies(h):
            out.wait_send()
            arriving.wait_recv()
            local.wait()

    for step in range(1, num_chips * CORES):
        peer = (me + step) % (num_chips * CORES)
        dw_out_to(step).wait_send()
        remote(dw_acc, dw_all.at[peer], dw_send.at[step], dw_recv.at[peer], chip, core).wait_recv()
    dw_out[...] = dw_all[...].sum(0).sum(1)


def attn_grads(num_chips, q, d_out, stats, kv, k_raw, cos_q, sin_q, cos_k, sin_k, wq, wk):
    kv_heads, _, rows, _ = q.shape
    chunk_len = kv.shape[3]
    heads = kv_heads // CORES
    half = (2, chunk_len, HEAD_DIM)
    bf16, f32 = jnp.bfloat16, jnp.float32
    sem = pltpu.SemaphoreType.DMA
    any_spec, vmem = pl.BlockSpec(memory_space=pl.ANY), pl.BlockSpec(memory_space=pltpu.VMEM)
    return pl.pallas_call(
        functools.partial(attn_kernel, num_chips),
        in_specs=[any_spec] * 4 + [vmem] * 7,
        out_specs=[any_spec, vmem, vmem, vmem],
        out_shape=[jax.ShapeDtypeStruct(q.shape, bf16), jax.ShapeDtypeStruct(k_raw.shape, bf16),
                   jax.ShapeDtypeStruct(k_raw.shape, bf16), jax.ShapeDtypeStruct((2, HEAD_DIM), f32)],
        scratch_shapes=[
            pltpu.VMEM((heads, 4, rows, HEAD_DIM), bf16),
            pltpu.VMEM((heads, 4, rows, HEAD_DIM), bf16),
            pltpu.VMEM((heads, 4) + stats.shape[2:], f32),
            pltpu.VMEM((num_chips, heads, 4) + half, bf16),
            pltpu.VMEM((4, rows, HEAD_DIM), bf16),
            pltpu.VMEM((4, HEAD_DIM, rows), bf16),
            pltpu.VMEM((4, HEAD_DIM, rows), bf16),
            pltpu.VMEM((4, HEAD_DIM, rows), f32),
            pltpu.VMEM((HEAD_DIM, chunk_len), bf16),
            pltpu.VMEM((chunk_len, rows), bf16),
            pltpu.VMEM((chunk_len, rows), bf16),
            pltpu.VMEM((4,) + half, f32),
            pltpu.VMEM((heads, 4) + half, f32),
            pltpu.VMEM((heads, 2) + half, f32),
            pltpu.VMEM((heads, 3, 4) + half, bf16),
            pltpu.VMEM((heads, 2, 4, chunk_len, HEAD_DIM), bf16),
            pltpu.VMEM((3, kv_heads, 2) + half, bf16),
            pltpu.VMEM(half, f32),
            pltpu.VMEM((2, 8, HEAD_DIM), f32),
            pltpu.VMEM((num_chips * CORES, 2, 8, HEAD_DIM), f32),
            sem((heads, 3, 2)), sem((heads, 3, 2)), sem((heads, 3, 2)),
            sem((heads, 2)), sem((heads, 2)), sem((heads, 2)),
            sem((heads, CORES, 2, 2)), sem((heads, 4, 2)),
            sem((heads, 2, 2)), sem((heads, 2, 2)),
            sem((heads, 2, 4)), sem((2, kv_heads, 2)),
            sem((heads, 2, 2)), sem((heads, 2, 2)),
            sem((heads, 4, 2)), sem((kv_heads, 2, 2)),
            sem((heads, 2)), sem((heads, 2)),
            sem((heads, 2)), sem((heads, 2)), sem((heads, 2)),
            sem((num_chips * CORES,)), sem((num_chips * CORES,)),
        ],
        compiler_params=pltpu.CompilerParams(vmem_limit_bytes=60 * 2 ** 20, collective_id=0, has_side_effects=True),
        cost_estimate=pl.CostEstimate(flops=50_000_000_000, bytes_accessed=64_000_000, transcendentals=40_000_000),
        name='attn_grads',
    )(q, d_out, stats, kv, k_raw, cos_q, sin_q, cos_k, sin_k, wq, wk)


def solution(mesh):
    cp_size = mesh.shape['cp']
    num_chips = cp_size // CORES

    def local_grads(q_raw, k_raw, v_proj, out_fwd, lse_fwd, d_out, q_norm, k_norm):
        dev_rank = lax.axis_index('cp')
        chip = dev_rank // CORES
        local_rows, num_heads = q_raw.shape[0], q_raw.shape[1]
        chunk_len = local_rows // 2
        kv_heads = k_raw.shape[1]
        per_kv = num_heads // kv_heads

        def by_head(arr):
            n = arr.shape[1] // kv_heads
            arr = arr.reshape((2, chunk_len, kv_heads, n) + arr.shape[2:])
            return jnp.moveaxis(arr, (2, 0, 3, 1), (0, 1, 2, 3))

        num_chunks = 2 * cp_size
        offsets = jnp.arange(chunk_len)
        chip_chunks = jnp.stack([2 * chip, 2 * chip + 1, num_chunks - 2 - 2 * chip, num_chunks - 1 - 2 * chip])
        cos_q, sin_q = rope_tables(chip_chunks[:, None] * chunk_len + offsets)
        dev_chunks = jnp.stack([dev_rank, num_chunks - 1 - dev_rank])
        cos_k, sin_k = rope_tables(dev_chunks[:, None] * chunk_len + offsets)

        delta = jnp.sum(d_out.astype(jnp.float32) * out_fwd.astype(jnp.float32), axis=-1)
        stats = jnp.stack([by_head(lse_fwd * LOG2E), by_head(delta)], axis=2)
        q_h = by_head(q_raw).reshape(kv_heads, 2, per_kv * chunk_len, HEAD_DIM)
        do_h = by_head(d_out).reshape(kv_heads, 2, per_kv * chunk_len, HEAD_DIM)
        k_h, v_h = by_head(k_raw)[:, :, 0], by_head(v_proj)[:, :, 0]
        raw = k_h.astype(jnp.float32)
        normed = raw * inverse_rms(raw) * k_norm
        key = normed * cos_k + jnp.concatenate([normed[..., HEAD_DIM // 2:], normed[..., :HEAD_DIM // 2]], axis=-1) * sin_k
        kv = jnp.stack([key.astype(jnp.bfloat16), v_h], axis=2)
        dq, dk, dv, weights = attn_grads(num_chips, q_h, do_h, stats, kv, k_h, cos_q, sin_q, cos_k, sin_k, q_norm[None], k_norm[None])

        def by_row(arr):
            arr = arr.reshape(kv_heads, 2, -1, chunk_len, HEAD_DIM)
            return jnp.moveaxis(arr, (1, 3, 0, 2), (0, 1, 2, 3)).reshape(local_rows, -1, HEAD_DIM)

        return by_row(dq), by_row(dk), by_row(dv), weights[0], weights[1]

    row_spec = P(('dp', 'cp'))
    in_specs = (row_spec, row_spec, row_spec, row_spec, row_spec, row_spec, P(), P())
    out_specs = (row_spec, row_spec, row_spec, P('dp'), P('dp'))
    return jax.shard_map(local_grads, mesh=mesh, in_specs=in_specs, out_specs=out_specs, check_vma=False)
```

time: 1170 us -> 223 us (0.19)
  waiting for transfers between devices: 461 us -> 0 us
  matrix products: 392 us -> 0 us
  Pallas kernels: 0 us -> 183 us
  other arithmetic: 141 us -> 14.9 us
  local copies, waits for them, and re-layouts: 113 us -> 23.1 us
  starting transfers between devices: 27.5 us -> 0 us
  blocking collectives: 21.9 us -> 0 us
    ppermute x30 -> x0, waiting for transfers between devices: 461 us -> none  [the longest x7 389 us: visit_source(): v_cur = lax.ppermute(v_cur, 'cp', shift_pairs)]
    dot_general x50 -> x0, matrix products: 392 us -> none  [the longest x10 90.7 us: pair_grads(): jnp.einsum('qngk,qngd->knd', prob_bf, do_blk, preferred_element_type=jnp....]
    pallas_call x0 -> x1, Pallas kernels: none -> 183 us  [attn_grads(): pl.pallas_call(functools.partial(attn_kernel, num_chips), in_specs=[any_s...]
    concatenate x10 -> x2, other arithmetic: 58.4 us -> 1.54 us  [rope_tables(): jnp.concatenate([cos_t, cos_t], axis=-1)]
    slice x28 -> x0, local copies, waits for them, and re-layouts: 46.8 us -> none  [the longest x6 28.1 us: late_source(): dq_acc[:chunk_len]]
    while x20 -> x0, local copies, waits for them, and re-layouts: 45.2 us -> none  [the longest x6 31.6 us: local_grads(): lax.fori_loop(1, cp_size, visit_source, (k_b, v_proj, dq_acc, dk_acc, dv_...]
    ppermute x30 -> x0, starting transfers between devices: 27.5 us -> none  [the longest x7 17.1 us: visit_source(): dv_cur = lax.ppermute(dv_cur, 'cp', shift_pairs)]
    psum x1 -> x0, blocking collectives: 21.9 us -> none  [local_grads(): lax.psum(dq_weight, 'cp')]
  transfers between devices with their start and end apart: 30 -> 0, of which waited for: 14 -> 0; matrix products, arithmetic and copies ran while one was open for 6% -> 0% of each run, Pallas kernels for 0% -> 0%
where the time goes in v2:
time: 223 us; the launch traced here: 222 us
  Pallas kernels  183 us (82%)
  local copies, waits for them, and re-layouts  23.1 us (10%)
  other arithmetic  14.9 us (7%)
    pallas_call x1, Pallas kernels, attn_grads(): pl.pallas_call(functools.partial(attn_kernel, num_chips), in_specs=[any_s...  183 us
    transpose x1, local copies, waits for them, and re-layouts, by_row(): jnp.moveaxis(arr, (1, 3, 0, 2), (0, 1, 2, 3))  7.53 us
    reshape x4, local copies, waits for them, and re-layouts, by_head(): arr = arr.reshape((2, chunk_len, kv_heads, n) + arr.shape[2:])  7.29 us
    reduce_sum x1, other arithmetic, local_grads(): jnp.sum(d_out.astype(jnp.float32) * out_fwd.astype(jnp.float32), axis=-1)  5.71 us
    unnamed x26, local copies, waits for them, and re-layouts  5.4 us

profile of v2, /device:TPU:81, one launch (start us, length us, event | category | flops | bytes accessed | tf_op | source)
XLA Modules:
  0.0 222.3 jit_solution(6076284282668057586)
XLA Ops:
  0.6 0.1 add_multiply_fusion.1
  0.7 0.1 add_multiply_fusion
  0.8 0.1 add_convert_fusion.1
  0.9 0.1 add_convert_fusion
  1.0 0.9 broadcast_multiply_fusion
  1.9 5.7 %multiply_reduce_fusion = f32[512,32]{1,0:T(8,128)S(1)} fusion(bf16[512,32,128]{2,1,0:T(8,128)(2,1)} %param.11, bf16[512,32,128]{2,1,0:T(8,128)(2,1)} %param.13), kind=kLoop, calls=%fused_computation | loop fusion | flops 8372224 | bytes 8454144 | tf_op jit(solution)/shard_map/reduce_sum | solution.py:507
  7.6 0.0 copy-start.3
  7.6 0.1 copy.34
  7.8 0.7 pad_maximum_fusion.5.st_hbm
  8.5 1.0 multiply_cosine_fusion.1
  9.5 0.0 copy-start.6
  9.5 0.2 pad_maximum_fusion.3
  9.7 0.1 copy.36
  9.9 0.0 copy-start.1
  9.9 0.6 fusion
  10.5 0.3 copy-done.6
  10.9 0.1 copy.37
  11.0 1.9 fusion.4
  12.9 1.3 pad_maximum_fusion.1
  14.3 0.6 fusion.1
  14.9 0.7 slice_bitcast_fusion.1
  15.6 1.4 fusion.3
  17.1 0.2 pad_maximum_fusion
  17.3 1.5 copy.38.kv_hbm
  18.8 1.4 copy-done.2
  20.2 3.6 %copy.31 = bf16[2,256,8,4,128]{4,1,3,0,2:T(8,128)(2,1)} copy(bf16[2,256,8,4,128]{4,3,2,1,0:T(4,128)(2,1)S(1)} %bitcast.63) | data formatting | bytes 8388608 | tf_op jit(solution)/shard_map/reshape | solution.py:497
  23.9 3.6 %copy.32 = bf16[2,256,8,4,128]{4,1,3,0,2:T(8,128)(2,1)} copy(bf16[2,256,8,4,128]{4,3,2,1,0:T(4,128)(2,1)S(1)} %bitcast.59) | data formatting | bytes 8388608 | tf_op jit(solution)/shard_map/reshape | solution.py:497
  27.4 183.4 %attn_grads.1 = (bf16[8,2,1024,128]{3,2,1,0:T(8,128)(2,1)}, bf16[8,2,256,128]{3,2,1,0:T(8,128)(2,1)}, bf16[8,2,256,128]{3,2,1,0:T(8,128)(2,1)}, f32[2,128]{1,0:T(2,128)}) custom-call(bf16[8,2,1024,128]{3,2,1,0:T(8,128)(2,1)} %bitcast.66, bf16[8,2,1024,128]{3,2,1,0:T(8,128)(2,1)} %bitcast.67, f32[8,2,2,4,256]{4,3,2,1,0:T(4,128)} %pad_maximum_fusion.5.st_hbm, ...), custom_call_target="tpu_custom_call" | custom-call | flops 49999998976 | bytes 64000000 | tf_op jit(solution)/shard_map/attn_grads/pallas_call | solution.py:439
  210.9 7.5 %copy.39 = bf16[2,256,8,4,128]{4,3,2,1,0:T(4,128)(2,1)} copy(bf16[2,256,8,4,128]{4,1,3,0,2:T(8,128)(2,1)} %bitcast.65) | data formatting | bytes 8388608 | tf_op jit(solution)/shard_map/transpose | solution.py:520
  218.4 1.6 copy.40
  220.1 0.5 slice_bitcast_fusion.2
  220.6 1.6 copy.41
  (22 shorter events, 0.2 us)
Async XLA Ops:
  7.6 2.1 copy-start.3
  9.5 1.4 copy-start.6
  9.7 5.9 %copy-start.4 = (f32[2,256,128]{2,1,0:T(8,128)}, f32[2,256,128]{2,1,0:T(8,128)S(1)}, u32[]{:S(2)}) copy-start(f32[2,256,128]{2,1,0:T(8,128)S(1)} %get-tuple-element.40.cos_k) | copy-start | bytes 786436
  9.7 5.9 %copy-start.5 = (f32[2,256,128]{2,1,0:T(8,128)}, f32[2,256,128]{2,1,0:T(8,128)S(1)}, u32[]{:S(2)}) copy-start(f32[2,256,128]{2,1,0:T(8,128)S(1)} %get-tuple-element.41.sin_k) | copy-start | bytes 786436
  9.9 5.8 %copy-start.1 = (bf16[512,8,128]{2,0,1:T(8,128)(2,1)}, bf16[512,8,128]{2,0,1:T(8,128)(2,1)S(1)}, u32[]{:S(2)}) copy-start(bf16[512,8,128]{2,0,1:T(8,128)(2,1)S(1)} %copy.36) | copy-start | bytes 3145732
  11.0 3.3 %copy-start.9 = (f32[128]{0:T(128)S(1)}, f32[128]{0:T(128)}, u32[]{:S(2)}) copy-start(f32[128]{0:T(128)} %param.15) | copy-start | bytes 1540
  17.3 2.9 %copy-start.2 = (bf16[512,32,128]{2,1,0:T(8,128)(2,1)S(1)}, bf16[512,32,128]{2,1,0:T(8,128)(2,1)}, u32[]{:S(2)}) copy-start(bf16[512,32,128]{2,1,0:T(8,128)(2,1)} %param.8) | copy-start | bytes 12582916
  20.2 3.6 %copy-start = (bf16[512,32,128]{2,1,0:T(8,128)(2,1)S(1)}, bf16[512,32,128]{2,1,0:T(8,128)(2,1)}, u32[]{:S(2)}) copy-start(bf16[512,32,128]{2,1,0:T(8,128)(2,1)} %param.13) | copy-start | bytes 12582916
  210.9 7.5 %copy-start.8 = (bf16[8,2,256,128]{3,2,1,0:T(8,128)(2,1)S(1)}, bf16[8,2,256,128]{3,2,1,0:T(8,128)(2,1)}, u32[]{:S(2)}) copy-start(bf16[8,2,256,128]{3,2,1,0:T(8,128)(2,1)} %get-tuple-element.10) | copy-start | bytes 3145732
  218.4 1.7 copy-start.10
  218.4 2.2 copy-start.7

commit v3 on v2

--- a/solution.py
+++ b/solution.py
@@ -41,14 +41,22 @@
     return grad_raw, weight_terms.reshape(-1, 8, HEAD_DIM).sum(0)
 
 
+def swap_rows(arr):
+    return jnp.concatenate([arr[HEAD_DIM // 2:], arr[:HEAD_DIM // 2]], axis=0)
+
+
+def inverse_rms_t(raw_in):
+    return lax.rsqrt(jnp.mean(raw_in * raw_in, axis=0, keepdims=True) + NORM_EPS)
+
+
 def dot(a, b):
     return lax.dot_general(a, b, (((1,), (0,)), ((), ())), preferred_element_type=jnp.float32)
 
 
 def attn_kernel(num_chips, q_hbm, do_hbm, st_hbm, kv_hbm, k_raw, cos_q, sin_q, cos_k, sin_k, wq, wk,
                 dq_hbm, dk_out, dv_out, dw_out,
-                q_buf, do_buf, st_buf, kv_buf, q_now, qt_now, dot_now, dqt_now, kt_now, p_now, ds_now,
-                acc, own_acc, own_recv, send_buf, transit, part, total, dw_acc, dw_all,
+                q_buf, do_buf, st_buf, kv_buf, raw_now, q_now, qt_now, dot_now, dqt_now, kt_now, p_now, ds_now,
+                acc, own_acc, own_recv, send_buf, transit, part, total, dwq_acc, dw_acc, dw_all,
                 ex_send, ex_recv, ex_local, own_send, own_kv_recv, own_local, nb_send, nb_recv, rl_send, op_recv,
                 pt_send, pt_recv, tr_send, tr_recv, fw_send, fw_recv, oa_send, oa_recv,
                 dq_send, dq_recv, dq_local, dw_send, dw_recv):
@@ -211,6 +219,173 @@
             def _(qb):
                 block(h, off, kc, qb, False)
 
+    def home(head, h, own):
+        for ch in range(2):
+            mine = place(core, ch)
+            total[...] = own_acc[h, mine] if own else own_recv[h, ch]
+
+            def add(slot):
+                total[...] += part[slot, head, ch].astype(jnp.float32)
+
+            def take_side(way):
+                remote(send_buf.at[0, 0, 0], part.at[2 * way, head, ch], pt_send.at[0, 0, 0], pt_recv.at[way, head, ch], left, core).wait_recv()
+                add(2 * way)
+
+            def take_far():
+                for kind in range(2):
+                    remote(transit.at[0, 0, 0], part.at[1, head, ch, kind], fw_send.at[0, 0, 0], fw_recv.at[head, ch, kind], left, core).wait_recv()
+                add(1)
+
+            if ch == 0:
+                take_side(0)
+                take_side(1)
+                take_far()
+            else:
+                @pl.when(right < chip)
+                def _():
+                    take_side(0)
+
+                @pl.when(left < chip)
+                def _():
+                    take_side(1)
+
+                @pl.when(far < chip)
+                def _():
+                    take_far()
+
+            raw = k_raw[head, ch].astype(jnp.float32)
+            grad_raw, terms = norm_rope_pull(raw, wk[...], cos_k[ch], sin_k[ch], total[0] * SM_SCALE)
+            dk_out[head, ch] = grad_raw.astype(jnp.bfloat16)
+            dv_out[head, ch] = total[1].astype(jnp.bfloat16)
+            dw_acc[1] += terms
+
+    def home_head(h):
+        for ch in range(2):
+            own_out(h, ch).wait_recv()
+            own_out(h, ch).wait_send()
+        home((1 - core) * heads + h, h, False)
+        home(core * heads + h, h, True)
+
+    def compute_head(h):
+        for copies in (own_copies(h), ex_copies(h)):
+            for out, arriving, local in copies:
+                out.wait_send()
+                arriving.wait_recv()
+                local.wait()
+        dqt_now[...] = jnp.zeros_like(dqt_now)
+
+        @pl.loop(0, num_chunks)
+        def _(qb):
+            for g in range(per_kv):
+                rows = pl.ds(g * chunk_len, chunk_len)
+                raw_bf = q_buf[h, qb, rows, :].T
+                raw_now[qb, :, rows] = raw_bf
+                raw = raw_bf.astype(jnp.float32)
+                normed = raw * inverse_rms_t(raw) * wq[...]
+                query = (normed * cos_q[qb] + swap_rows(normed) * sin_q[qb]).astype(jnp.bfloat16)
+                qt_now[qb, :, rows] = query
+                q_now[qb, rows, :] = query.T
+            dot_now[qb] = do_buf[h, qb].T
+
+        last = h == heads - 1
+
+        @pl.loop(0, num_chips)
+        def _(j):
+            first_order = jnp.where(j == 0, 0, jnp.where(j == 1, 1, jnp.where(j == 2, 3, 2)))
+            last_order = jnp.where(j == 0, 2, jnp.where(j == 1, 1, jnp.where(j == 2, 3, 0)))
+            off = jnp.where(last, last_order, first_order)
+
+            @pl.when(off == 2)
+            def _():
+                for kind in range(2):
+                    relay(h, 0, kind).wait_recv()
+
+                @pl.when(chip < far)
+                def _():
+                    for kind in range(2):
+                        relay(h, 1, kind).wait_recv()
+
+            source_block(h, off)
+            src = (chip + off) % num_chips
+
+            @pl.when(off == 0)
+            def _():
+                own_acc[h] = acc[...]
+                for ch in range(2):
+                    own_out(h, ch).start()
+
+            @pl.when(off != 0)
+            def _():
+                send_buf[h, off - 1, 0:2] = acc[0:2].astype(jnp.bfloat16)
+
+                @pl.when(chip < src)
+                def _():
+                    send_buf[h, off - 1, 2:4] = acc[2:4].astype(jnp.bfloat16)
+
+            for side in (1, 3):
+                @pl.when(off == side)
+                def _():
+                    part_out(h, side, 0).start()
+                    part_out(h, side, 1).start()
+
+                    @pl.when(chip < src)
+                    def _():
+                        part_out(h, side, 2).start()
+                        part_out(h, side, 3).start()
+
+            @pl.when(off == 2)
+            def _():
+                for kind in range(2):
+                    transit_out(h, 0, kind).start()
+
+                @pl.when(chip < src)
+                def _():
+                    for kind in range(2):
+                        transit_out(h, 1, kind).start()
+
+            def pass_keys(of_head):
+                nb_wait(of_head, 0)
+                nb_wait(of_head, 1)
+                relay_each(of_head, lambda copy: copy.start())
+
+                @pl.when(of_head + 2 < heads)
+                def _():
+                    nb_each(of_head + 2, lambda copy: copy.start())
+
+            @pl.when((h == 0) & (j == 0))
+            def _():
+                pass_keys(0)
+
+            @pl.when((j == 3) & (h + 1 < heads))
+            def _():
+                pass_keys(h + 1)
+
+            @pl.when((j == 0) & (h > 0))
+            def _():
+                forward_each(h - 1, start_forward)
+
+            @pl.when((j == 2) & last)
+            def _():
+                forward_each(h, start_forward)
+
+        @pl.loop(0, num_chunks)
+        def _(qb):
+            for g in range(per_kv):
+                rows = pl.ds(g * chunk_len, chunk_len)
+                grad = dqt_now[qb, :, rows] * SM_SCALE
+                raw = raw_now[qb, :, rows].astype(jnp.float32)
+                inv_rms = inverse_rms_t(raw)
+                unit = raw * inv_rms
+                grad_normed = grad * cos_q[qb] - swap_rows(grad) * sin_q[qb]
+                dwq_acc[...] += grad_normed * unit
+                grad_unit = grad_normed * wq[...]
+                grad_raw = inv_rms * (grad_unit - unit * jnp.mean(grad_unit * unit, axis=0, keepdims=True))
+                q_buf[h, qb, rows, :] = grad_raw.astype(jnp.bfloat16).T
+
+        for out, _, local in dq_copies(h):
+            out.start()
+            local.start()
+
     barrier = pltpu.get_barrier_semaphore()
     for step in range(1, num_chips * CORES):
         pl.semaphore_signal(barrier, inc=1, device_id={'cp': (me + step) % (num_chips * CORES)}, device_id_type=MESH)
@@ -227,171 +402,22 @@
             out.start()
             local.start()
 
+    nb_each(1, lambda copy: copy.start())
+
     dw_acc[...] = jnp.zeros_like(dw_acc)
-
-    @pl.loop(0, heads)
+    dwq_acc[...] = jnp.zeros_like(dwq_acc)
+
+    @pl.loop(0, heads + 2)
     def _(h):
-        for copies in (own_copies(h), ex_copies(h)):
-            for out, arriving, local in copies:
-                out.wait_send()
-                arriving.wait_recv()
-                local.wait()
-        dqt_now[...] = jnp.zeros_like(dqt_now)
-
-        @pl.loop(0, num_chunks)
-        def _(qb):
-            for g in range(per_kv):
-                rows = pl.ds(g * chunk_len, chunk_len)
-                raw = q_buf[h, qb, rows, :].astype(jnp.float32)
-                normed = raw * inverse_rms(raw) * wq[...]
-                query = (normed * cos_q[qb] + swap_halves(normed) * sin_q[qb]).astype(jnp.bfloat16)
-                q_now[qb, rows, :] = query
-                qt_now[qb, :, rows] = query.T
-            dot_now[qb] = do_buf[h, qb].T
-
-        last = h == heads - 1
-
-        @pl.loop(0, num_chips)
-        def _(j):
-            first_order = jnp.where(j == 0, 0, jnp.where(j == 1, 1, jnp.where(j == 2, 3, 2)))
-            last_order = jnp.where(j == 0, 2, jnp.where(j == 1, 1, jnp.where(j == 2, 3, 0)))
-            off = jnp.where(last, last_order, first_order)
-
-            @pl.when(off == 2)
-            def _():
-                for kind in range(2):
-                    relay(h, 0, kind).wait_recv()
-
-                @pl.when(chip < far)
-                def _():
-                    for kind in range(2):
-                        relay(h, 1, kind).wait_recv()
-
-            source_block(h, off)
-            src = (chip + off) % num_chips
-
-            @pl.when(off == 0)
-            def _():
-                own_acc[h] = acc[...]
-                for ch in range(2):
-                    own_out(h, ch).start()
-
-            @pl.when(off != 0)
-            def _():
-                send_buf[h, off - 1, 0:2] = acc[0:2].astype(jnp.bfloat16)
-
-                @pl.when(chip < src)
-                def _():
-                    send_buf[h, off - 1, 2:4] = acc[2:4].astype(jnp.bfloat16)
-
-            for side in (1, 3):
-                @pl.when(off == side)
-                def _():
-                    part_out(h, side, 0).start()
-                    part_out(h, side, 1).start()
-
-                    @pl.when(chip < src)
-                    def _():
-                        part_out(h, side, 2).start()
-                        part_out(h, side, 3).start()
-
-            @pl.when(off == 2)
-            def _():
-                for kind in range(2):
-                    transit_out(h, 0, kind).start()
-
-                @pl.when(chip < src)
-                def _():
-                    for kind in range(2):
-                        transit_out(h, 1, kind).start()
-
-            def pass_keys(of_head):
-                nb_wait(of_head, 0)
-                nb_wait(of_head, 1)
-                relay_each(of_head, lambda copy: copy.start())
-
-                @pl.when(of_head + 1 < heads)
-                def _():
-                    nb_each(of_head + 1, lambda copy: copy.start())
-
-            @pl.when((h == 0) & (j == 0))
-            def _():
-                pass_keys(0)
-
-            @pl.when((j == 2) & (h + 1 < heads))
-            def _():
-                pass_keys(h + 1)
-
-            @pl.when((j == 0) & (h > 0))
-            def _():
-                forward_each(h - 1, start_forward)
-
-            @pl.when((j == 2) & last)
-            def _():
-                forward_each(h, start_forward)
-
-        @pl.loop(0, num_chunks)
-        def _(qb):
-            for g in range(per_kv):
-                rows = pl.ds(g * chunk_len, chunk_len)
-                grad = dqt_now[qb, :, rows].T * SM_SCALE
-                raw = q_buf[h, qb, rows, :].astype(jnp.float32)
-                grad_raw, terms = norm_rope_pull(raw, wq[...], cos_q[qb], sin_q[qb], grad)
-                q_buf[h, qb, rows, :] = grad_raw.astype(jnp.bfloat16)
-                dw_acc[0] += terms
-
-        for out, _, local in dq_copies(h):
-            out.start()
-            local.start()
-
-    def home(head, h, own):
-        for ch in range(2):
-            mine = place(core, ch)
-            total[...] = own_acc[h, mine] if own else own_recv[h, ch]
-
-            def add(slot):
-                total[...] += part[slot, head, ch].astype(jnp.float32)
-
-            def take_side(way):
-                remote(send_buf.at[0, 0, 0], part.at[2 * way, head, ch], pt_send.at[0, 0, 0], pt_recv.at[way, head, ch], left, core).wait_recv()
-                add(2 * way)
-
-            def take_far():
-                for kind in range(2):
-                    remote(transit.at[0, 0, 0], part.at[1, head, ch, kind], fw_send.at[0, 0, 0], fw_recv.at[head, ch, kind], left, core).wait_recv()
-                add(1)
-
-            if ch == 0:
-                take_side(0)
-                take_side(1)
-                take_far()
-            else:
-                @pl.when(right < chip)
-                def _():
-                    take_side(0)
-
-                @pl.when(left < chip)
-                def _():
-                    take_side(1)
-
-                @pl.when(far < chip)
-                def _():
-                    take_far()
-
-            raw = k_raw[head, ch].astype(jnp.float32)
-            grad_raw, terms = norm_rope_pull(raw, wk[...], cos_k[ch], sin_k[ch], total[0] * SM_SCALE)
-            dk_out[head, ch] = grad_raw.astype(jnp.bfloat16)
-            dv_out[head, ch] = total[1].astype(jnp.bfloat16)
-            dw_acc[1] += terms
-
-    @pl.loop(0, heads)
-    def _(h):
-        for ch in range(2):
-            own_out(h, ch).wait_recv()
-            own_out(h, ch).wait_send()
-        home((1 - core) * heads + h, h, False)
-        home(core * heads + h, h, True)
-
+        @pl.when(h < heads)
+        def _():
+            compute_head(h)
+
+        @pl.when(h >= 2)
+        def _():
+            home_head(h - 2)
+
+    dw_acc[0] = dwq_acc[...].T.reshape(-1, 8, HEAD_DIM).sum(0)
     for step in range(1, num_chips * CORES):
         dw_out_to(step).start()
     dw_all[me] = dw_acc[...]
@@ -426,6 +452,81 @@
         dw_out_to(step).wait_send()
         remote(dw_acc, dw_all.at[peer], dw_send.at[step], dw_recv.at[peer], chip, core).wait_recv()
     dw_out[...] = dw_all[...].sum(0).sum(1)
+
+
+def prepare_kernel(q_ref, do_ref, out_ref, k_ref, v_ref, lse_ref, cos_k, sin_k, wk, q_out, do_out, st_out, kv_out, k_out):
+    rows, num_heads = q_ref.shape[0], q_ref.shape[1]
+    kv_heads = k_ref.shape[1]
+    f32, bf16 = jnp.float32, jnp.bfloat16
+
+    def by_head(arr):
+        return jnp.swapaxes(arr, 0, 1)
+
+    d_out = do_ref[...].astype(f32)
+    q_out[:, 0] = by_head(q_ref[...].astype(f32)).astype(bf16).reshape(kv_heads, -1, rows, HEAD_DIM)
+    do_out[:, 0] = by_head(d_out).astype(bf16).reshape(kv_heads, -1, rows, HEAD_DIM)
+    delta = jnp.sum(d_out * out_ref[...].astype(f32), axis=-1)
+    st_out[:, 0, 0] = (lse_ref[...] * LOG2E).T.reshape(kv_heads, -1, rows)
+    st_out[:, 0, 1] = delta.T.reshape(kv_heads, -1, rows)
+    raw = k_ref[...].astype(f32)
+    normed = raw * inverse_rms(raw) * wk[...]
+    key = normed * cos_k[0][:, None] + swap_halves(normed) * sin_k[0][:, None]
+    kv_out[:, 0, 0] = by_head(key).astype(bf16)
+    kv_out[:, 0, 1] = by_head(v_ref[...].astype(f32)).astype(bf16)
+    k_out[:, 0] = by_head(raw).astype(bf16)
+
+
+def prepare(q_raw, d_out, out_fwd, k_raw, v_proj, lse_fwd, cos_k, sin_k, wk, rows=128):
+    local_rows, num_heads, _ = q_raw.shape
+    kv_heads = k_raw.shape[1]
+    per_kv, chunk_len = num_heads // kv_heads, local_rows // 2
+    parts = chunk_len // rows
+    bf16 = jnp.bfloat16
+    rows_q = pl.BlockSpec((rows, num_heads, HEAD_DIM), lambda i: (i, 0, 0))
+    rows_k = pl.BlockSpec((rows, kv_heads, HEAD_DIM), lambda i: (i, 0, 0))
+    table = pl.BlockSpec((1, rows, HEAD_DIM), lambda i: (i // parts, i % parts, 0))
+    heads_q = pl.BlockSpec((kv_heads, 1, per_kv, rows, HEAD_DIM), lambda i: (0, i // parts, 0, i % parts, 0))
+    return pl.pallas_call(
+        prepare_kernel,
+        grid=(2 * parts,),
+        in_specs=[rows_q, rows_q, rows_q, rows_k, rows_k, pl.BlockSpec((rows, num_heads), lambda i: (i, 0)), table, table,
+                  pl.BlockSpec((1, HEAD_DIM), lambda i: (0, 0))],
+        out_specs=[heads_q, heads_q,
+                   pl.BlockSpec((kv_heads, 1, 2, per_kv, rows), lambda i: (0, i // parts, 0, 0, i % parts)),
+                   pl.BlockSpec((kv_heads, 1, 2, rows, HEAD_DIM), lambda i: (0, i // parts, 0, i % parts, 0)),
+                   pl.BlockSpec((kv_heads, 1, rows, HEAD_DIM), lambda i: (0, i // parts, i % parts, 0))],
+        out_shape=[jax.ShapeDtypeStruct((kv_heads, 2, per_kv, chunk_len, HEAD_DIM), bf16),
+                   jax.ShapeDtypeStruct((kv_heads, 2, per_kv, chunk_len, HEAD_DIM), bf16),
+                   jax.ShapeDtypeStruct((kv_heads, 2, 2, per_kv, chunk_len), jnp.float32),
+                   jax.ShapeDtypeStruct((kv_heads, 2, 2, chunk_len, HEAD_DIM), bf16),
+                   jax.ShapeDtypeStruct((kv_heads, 2, chunk_len, HEAD_DIM), bf16)],
+        compiler_params=pltpu.CompilerParams(vmem_limit_bytes=48 * 2 ** 20),
+        name='prepare',
+    )(q_raw, d_out, out_fwd, k_raw, v_proj, lse_fwd, cos_k, sin_k, wk)
+
+
+def finish_kernel(dq_ref, dk_ref, dv_ref, dq_out, dk_out, dv_out):
+    for src, dst in ((dq_ref, dq_out), (dk_ref, dk_out), (dv_ref, dv_out)):
+        by_head = src[:, 0].reshape(-1, src.shape[-2], HEAD_DIM).astype(jnp.float32)
+        dst[...] = jnp.swapaxes(by_head, 0, 1).astype(jnp.bfloat16)
+
+
+def finish(dq, dk, dv, rows=128):
+    kv_heads, _, per_kv, chunk_len, _ = dq.shape
+    parts = chunk_len // rows
+    num_heads = kv_heads * per_kv
+    heads_k = pl.BlockSpec((kv_heads, 1, rows, HEAD_DIM), lambda i: (0, i // parts, i % parts, 0))
+    rows_k = pl.BlockSpec((rows, kv_heads, HEAD_DIM), lambda i: (i, 0, 0))
+    out_k = jax.ShapeDtypeStruct((2 * chunk_len, kv_heads, HEAD_DIM), jnp.bfloat16)
+    return pl.pallas_call(
+        finish_kernel,
+        grid=(2 * parts,),
+        in_specs=[pl.BlockSpec((kv_heads, 1, per_kv, rows, HEAD_DIM), lambda i: (0, i // parts, 0, i % parts, 0)), heads_k, heads_k],
+        out_specs=[pl.BlockSpec((rows, num_heads, HEAD_DIM), lambda i: (i, 0, 0)), rows_k, rows_k],
+        out_shape=[jax.ShapeDtypeStruct((2 * chunk_len, num_heads, HEAD_DIM), jnp.bfloat16), out_k, out_k],
+        compiler_params=pltpu.CompilerParams(vmem_limit_bytes=48 * 2 ** 20),
+        name='finish',
+    )(dq, dk, dv)
 
 
 def attn_grads(num_chips, q, d_out, stats, kv, k_raw, cos_q, sin_q, cos_k, sin_k, wq, wk):
@@ -447,6 +548,7 @@
             pltpu.VMEM((heads, 4, rows, HEAD_DIM), bf16),
             pltpu.VMEM((heads, 4) + stats.shape[2:], f32),
             pltpu.VMEM((num_chips, heads, 4) + half, bf16),
+            pltpu.VMEM((4, HEAD_DIM, rows), bf16),
             pltpu.VMEM((4, rows, HEAD_DIM), bf16),
             pltpu.VMEM((4, HEAD_DIM, rows), bf16),
             pltpu.VMEM((4, HEAD_DIM, rows), bf16),
@@ -461,6 +563,7 @@
             pltpu.VMEM((heads, 2, 4, chunk_len, HEAD_DIM), bf16),
             pltpu.VMEM((3, kv_heads, 2) + half, bf16),
             pltpu.VMEM(half, f32),
+            pltpu.VMEM((HEAD_DIM, chunk_len), f32),
             pltpu.VMEM((2, 8, HEAD_DIM), f32),
             pltpu.VMEM((num_chips * CORES, 2, 8, HEAD_DIM), f32),
             sem((heads, 3, 2)), sem((heads, 3, 2)), sem((heads, 3, 2)),
@@ -492,11 +595,6 @@
         kv_heads = k_raw.shape[1]
         per_kv = num_heads // kv_heads
 
-        def by_head(arr):
-            n = arr.shape[1] // kv_heads
-            arr = arr.reshape((2, chunk_len, kv_heads, n) + arr.shape[2:])
-            return jnp.moveaxis(arr, (2, 0, 3, 1), (0, 1, 2, 3))
-
         num_chunks = 2 * cp_size
         offsets = jnp.arange(chunk_len)
         chip_chunks = jnp.stack([2 * chip, 2 * chip + 1, num_chunks - 2 - 2 * chip, num_chunks - 1 - 2 * chip])
@@ -504,22 +602,14 @@
         dev_chunks = jnp.stack([dev_rank, num_chunks - 1 - dev_rank])
         cos_k, sin_k = rope_tables(dev_chunks[:, None] * chunk_len + offsets)
 
-        delta = jnp.sum(d_out.astype(jnp.float32) * out_fwd.astype(jnp.float32), axis=-1)
-        stats = jnp.stack([by_head(lse_fwd * LOG2E), by_head(delta)], axis=2)
-        q_h = by_head(q_raw).reshape(kv_heads, 2, per_kv * chunk_len, HEAD_DIM)
-        do_h = by_head(d_out).reshape(kv_heads, 2, per_kv * chunk_len, HEAD_DIM)
-        k_h, v_h = by_head(k_raw)[:, :, 0], by_head(v_proj)[:, :, 0]
-        raw = k_h.astype(jnp.float32)
-        normed = raw * inverse_rms(raw) * k_norm
-        key = normed * cos_k + jnp.concatenate([normed[..., HEAD_DIM // 2:], normed[..., :HEAD_DIM // 2]], axis=-1) * sin_k
-        kv = jnp.stack([key.astype(jnp.bfloat16), v_h], axis=2)
-        dq, dk, dv, weights = attn_grads(num_chips, q_h, do_h, stats, kv, k_h, cos_q, sin_q, cos_k, sin_k, q_norm[None], k_norm[None])
-
-        def by_row(arr):
-            arr = arr.reshape(kv_heads, 2, -1, chunk_len, HEAD_DIM)
-            return jnp.moveaxis(arr, (1, 3, 0, 2), (0, 1, 2, 3)).reshape(local_rows, -1, HEAD_DIM)
-
-        return by_row(dq), by_row(dk), by_row(dv), weights[0], weights[1]
+        q_h, do_h, stats, kv, k_h = prepare(q_raw, d_out, out_fwd, k_raw, v_proj, lse_fwd, cos_k, sin_k, k_norm[None])
+        stacked = (kv_heads, 2, per_kv * chunk_len, HEAD_DIM)
+        cos_qt, sin_qt = jnp.swapaxes(cos_q, 1, 2), jnp.swapaxes(sin_q, 1, 2)
+        wq_t = jnp.broadcast_to(q_norm[:, None], (HEAD_DIM, chunk_len))
+        dq, dk, dv, weights = attn_grads(num_chips, q_h.reshape(stacked), do_h.reshape(stacked), stats, kv, k_h,
+                                         cos_qt, sin_qt, cos_k, sin_k, wq_t, k_norm[None])
+        dq_raw, dk_raw, dv_home = finish(dq.reshape(q_h.shape), dk, dv)
+        return dq_raw, dk_raw, dv_home, weights[0], weights[1]
 
     row_spec = P(('dp', 'cp'))
     in_specs = (row_spec, row_spec, row_spec, row_spec, row_spec, row_spec, P(), P())

time: 223 us -> 200 us (0.90)
  local copies, waits for them, and re-layouts: 23.1 us -> 8.51 us
  other arithmetic: 14.9 us -> 3.59 us
  Pallas kernels: 183 us -> 187 us
    pallas_call x0 -> x2, Pallas kernels: none -> 18.4 us  [the longest x1 12.2 us: prepare(): pl.pallas_call(prepare_kernel, grid=(2 * parts,), in_specs=[rows_q, rows_...]
    pallas_call x1, Pallas kernels: 183 us -> 168 us  [attn_grads(): pl.pallas_call(functools.partial(attn_kernel, num_chips), in_specs=[any_s...]
    transpose x1 -> x0, local copies, waits for them, and re-layouts: 7.53 us -> none  [by_row(): jnp.moveaxis(arr, (1, 3, 0, 2), (0, 1, 2, 3))]
    reshape x4 -> x0, local copies, waits for them, and re-layouts: 7.29 us -> none  [by_head(): arr = arr.reshape((2, chunk_len, kv_heads, n) + arr.shape[2:])]
    reduce_sum x2 -> x0, other arithmetic: 6.34 us -> none  [the longest x1 5.71 us: local_grads(): jnp.sum(d_out.astype(jnp.float32) * out_fwd.astype(jnp.float32), axis=-1)]
    unnamed x26 -> x23, local copies, waits for them, and re-layouts: 5.4 us -> 6.42 us
where the time goes in v3:
time: 200 us
  Pallas kernels  187 us (94%)
  local copies, waits for them, and re-layouts  8.51 us (4%)
  other arithmetic  3.59 us (2%)
    pallas_call x1, Pallas kernels, attn_grads(): pl.pallas_call(functools.partial(attn_kernel, num_chips), in_specs=[any_s...  168 us
    pallas_call x1, Pallas kernels, prepare(): pl.pallas_call(prepare_kernel, grid=(2 * parts,), in_specs=[rows_q, rows_...  12.2 us
    unnamed x23, local copies, waits for them, and re-layouts  6.42 us
    pallas_call x1, Pallas kernels, finish(): pl.pallas_call(finish_kernel, grid=(2 * parts,), in_specs=[pl.BlockSpec((...  6.24 us

profile of v3, /device:TPU:81, one launch (start us, length us, event | category | flops | bytes accessed | tf_op | source)
XLA Modules:
  0.0 199.7 jit_solution(13212042185398579038)
XLA Ops:
  0.6 0.0 copy-start.6
  0.6 0.0 copy-start.3
  0.7 0.0 copy-start.2
  0.7 0.1 add_multiply_fusion.1
  0.8 0.1 add_multiply_fusion
  0.8 0.1 add_convert_fusion.1
  0.9 0.1 add_convert_fusion
  1.0 1.6 broadcast_in_dim.5.wq
  2.6 1.0 copy.13.lse_ref
  3.5 1.0 fusion.1
  4.5 1.1 maximum_bitcast_fusion
  5.6 1.0 fusion
  6.6 0.2 pad_maximum_fusion
  6.8 0.0 copy-start
  6.8 0.0 copy-start.1
  6.9 0.0 copy-done.6
  6.9 0.0 copy-done.3
  6.9 0.0 copy-done.2
  6.9 12.2 %prepare.1 = (bf16[8,2,4,256,128]{4,3,2,1,0:T(8,128)(2,1)}, bf16[8,2,4,256,128]{4,3,2,1,0:T(8,128)(2,1)}, f32[8,2,2,4,256]{4,3,2,1,0:T(4,128)S(1)}, bf16[8,2,2,2...) custom-call(bf16[512,32,128]{2,1,0:T(8,128)(2,1)} %q_ref.1, bf16[512,32,128]{2,1,0:T(8,128)(2,1)} %do_ref.1, ...), custom_call_target="tpu_custom_call" | custom-call | tf_op jit(solution)/shard_map/prepare/pallas_call | solution.py:489
  19.1 0.0 copy-done
  19.1 0.0 copy-done.1
  19.1 0.0 copy-start.7
  19.1 1.4 copy-done.7
  20.5 1.0 copy-done.8
  21.4 0.6 copy-done.9
  22.1 168.4 %attn_grads.1 = (bf16[8,2,1024,128]{3,2,1,0:T(8,128)(2,1)}, bf16[8,2,256,128]{3,2,1,0:T(8,128)(2,1)}, bf16[8,2,256,128]{3,2,1,0:T(8,128)(2,1)}, f32[2,128]{1,0:T(2,128)}) custom-call(bf16[8,2,1024,128]{3,2,1,0:T(8,128)(2,1)} %bitcast.21, bf16[8,2,1024,128]{3,2,1,0:T(8,128)(2,1)} %bitcast.22, f32[8,2,2,4,256]{4,3,2,1,0:T(4,128)} %copy-done.9, ...), custom_call_target="tpu_custom_call" | custom-call | flops 49999998976 | bytes 64000000 | tf_op jit(solution)/shard_map/attn_grads/pallas_call | solution.py:540
  190.5 0.0 copy-start.10
  190.5 0.0 copy-start.4
  190.5 1.2 copy-done.4
  191.8 1.2 copy-done.5
  193.0 6.2 %finish.1 = (bf16[512,32,128]{2,1,0:T(8,128)(2,1)}, bf16[512,8,128]{2,1,0:T(8,128)(2,1)}, bf16[512,8,128]{2,1,0:T(8,128)(2,1)}) custom-call(bf16[8,2,4,256,128]{4,3,2,1,0:T(8,128)(2,1)} %bitcast.20, bf16[8,2,256,128]{3,2,1,0:T(8,128)(2,1)S(1)} %copy-done.4, bf16[8,2,256,128]{3,2,1,0:T(8,128)(2,1)S(1)} %copy-done.5), custom_call_target="tpu_custom_call" | custom-call | tf_op jit(solution)/shard_map/finish/pallas_call | solution.py:521
  199.2 0.5 slice_bitcast_fusion
  (5 shorter events, 0.0 us)
Async XLA Ops:
  0.6 6.2 %copy-start.6 = (f32[128]{0:T(128)S(1)}, f32[128]{0:T(128)}, u32[]{:S(2)}) copy-start(f32[128]{0:T(128)} %param.15) | copy-start | bytes 1540
  0.6 6.2 %copy-start.3 = (bf16[512,8,128]{2,1,0:T(8,128)(2,1)S(1)}, bf16[512,8,128]{2,1,0:T(8,128)(2,1)}, u32[]{:S(2)}) copy-start(bf16[512,8,128]{2,1,0:T(8,128)(2,1)} %v_ref.1) | copy-start | bytes 3145732
  0.7 6.2 %copy-start.2 = (bf16[512,8,128]{2,1,0:T(8,128)(2,1)S(1)}, bf16[512,8,128]{2,1,0:T(8,128)(2,1)}, u32[]{:S(2)}) copy-start(bf16[512,8,128]{2,1,0:T(8,128)(2,1)} %k_ref.1) | copy-start | bytes 3145732
  6.8 12.2 %copy-start = (f32[2,256,128]{2,1,0:T(8,128)}, f32[2,256,128]{2,1,0:T(8,128)S(1)}, u32[]{:S(2)}) copy-start(f32[2,256,128]{2,1,0:T(8,128)S(1)} %get-tuple-element.37.cos_k) | copy-start | bytes 786436
  6.8 12.2 %copy-start.1 = (f32[2,256,128]{2,1,0:T(8,128)}, f32[2,256,128]{2,1,0:T(8,128)S(1)}, u32[]{:S(2)}) copy-start(f32[2,256,128]{2,1,0:T(8,128)S(1)} %get-tuple-element.38.sin_k) | copy-start | bytes 786436
  19.1 1.4 copy-start.7
  20.5 1.0 copy-start.8
  21.4 0.6 copy-start.9
  190.5 8.7 %copy-start.10 = (f32[2,128]{1,0:T(2,128)S(1)}, f32[2,128]{1,0:T(2,128)}, u32[]{:S(2)}) copy-start(f32[2,128]{1,0:T(2,128)} %get-tuple-element.28) | copy-start | bytes 3076
  190.5 1.2 copy-start.4
  191.8 1.2 copy-start.5

commit v4 on v3

--- a/solution.py
+++ b/solution.py
@@ -53,13 +53,14 @@
     return lax.dot_general(a, b, (((1,), (0,)), ((), ())), preferred_element_type=jnp.float32)
 
 
-def attn_kernel(num_chips, q_hbm, do_hbm, st_hbm, kv_hbm, k_raw, cos_q, sin_q, cos_k, sin_k, wq, wk,
-                dq_hbm, dk_out, dv_out, dw_out,
+def attn_kernel(num_chips, q_hbm, do_hbm, st_hbm, kv_hbm, k_hbm, tables_hbm, k_tables_hbm, wq_row, wk,
+                dq_hbm, dkv_hbm, dw_out,
+                k_raw, tables, k_tables, wq, dkv_out,
                 q_buf, do_buf, st_buf, kv_buf, raw_now, q_now, qt_now, dot_now, dqt_now, kt_now, p_now, ds_now,
                 acc, own_acc, own_recv, send_buf, transit, part, total, dwq_acc, dw_acc, dw_all,
                 ex_send, ex_recv, ex_local, own_send, own_kv_recv, own_local, nb_send, nb_recv, rl_send, op_recv,
                 pt_send, pt_recv, tr_send, tr_recv, fw_send, fw_recv, oa_send, oa_recv,
-                dq_send, dq_recv, dq_local, dw_send, dw_recv):
+                dq_send, dq_recv, dq_local, dw_send, dw_recv, in_local, out_local):
     me = lax.axis_index('cp')
     chip, core = me // CORES, me % CORES
     left, right = (chip + num_chips - 1) % num_chips, (chip + 1) % num_chips
@@ -67,6 +68,15 @@
     heads = q_buf.shape[0]
     num_chunks, chunk_len = kv_buf.shape[2], kv_buf.shape[4]
     per_kv = q_buf.shape[2] // chunk_len
+    cos_q, sin_q = tables.at[0], tables.at[1]
+    cos_k, sin_k = k_tables.at[0], k_tables.at[1]
+
+    def in_copy(i):
+        src, dst = ((tables_hbm, tables), (k_tables_hbm, k_tables), (k_hbm, k_raw))[i]
+        return pltpu.make_async_copy(src, dst, in_local.at[i])
+
+    def out_copy(head):
+        return pltpu.make_async_copy(dkv_out.at[head], dkv_hbm.at[head], out_local.at[head])
 
     def remote(src, dst, send_sem, recv_sem, to_chip, to_core):
         return pltpu.make_async_remote_copy(src_ref=src, dst_ref=dst, send_sem=send_sem, recv_sem=recv_sem,
@@ -182,7 +192,7 @@
         peer = (me + step) % (num_chips * CORES)
         return remote(dw_acc, dw_all.at[me], dw_send.at[step], dw_recv.at[me], peer // CORES, peer % CORES)
 
-    def block(h, off, kc, qb, masked):
+    def block(h, off, kc, qb, masked, slot=0):
         k_blk, v_blk = kv_buf[off, h, kc, 0], kv_buf[off, h, kc, 1]
         if masked:
             key_pos = lax.broadcasted_iota(jnp.int32, (chunk_len, chunk_len), 0)
@@ -195,11 +205,11 @@
                 logits = jnp.where(visible, logits, -jnp.inf)
             prob = jnp.exp2(logits)
             dprob = dot(v_blk, dot_now[qb, :, cols])
-            p_now[:, cols] = prob.astype(jnp.bfloat16)
-            ds_now[:, cols] = (prob * (dprob - st_buf[h, qb, 1, g:g + 1, :])).astype(jnp.bfloat16)
-        acc[kc, 1] += dot(p_now[...], do_buf[h, qb])
-        acc[kc, 0] += dot(ds_now[...], q_now[qb])
-        dqt_now[qb] += dot(kt_now[...], ds_now[...])
+            p_now[slot, :, cols] = prob.astype(jnp.bfloat16)
+            ds_now[slot, :, cols] = (prob * (dprob - st_buf[h, qb, 1, g:g + 1, :])).astype(jnp.bfloat16)
+        acc[kc, 1] += dot(p_now[slot], do_buf[h, qb])
+        acc[kc, 0] += dot(ds_now[slot], q_now[qb])
+        dqt_now[qb] += dot(kt_now[...], ds_now[slot])
 
     def source_block(h, off):
         src = (chip + off) % num_chips
@@ -215,9 +225,16 @@
             def _():
                 block(h, off, kc, kc, True)
 
-            @pl.loop(jnp.where(own, kc + 1, jnp.where(early, 0, num_chunks // 2)), num_chunks)
-            def _(qb):
-                block(h, off, kc, qb, False)
+                @pl.loop(kc + 1, num_chunks)
+                def _(qb):
+                    block(h, off, kc, qb, False)
+
+            @pl.when(jnp.logical_not(own))
+            def _():
+                @pl.loop(jnp.where(early, 0, num_chunks // 4), num_chunks // 2)
+                def _(pair):
+                    block(h, off, kc, 2 * pair, False)
+                    block(h, off, kc, 2 * pair + 1, False, 1)
 
     def home(head, h, own):
         for ch in range(2):
@@ -255,9 +272,10 @@
 
             raw = k_raw[head, ch].astype(jnp.float32)
             grad_raw, terms = norm_rope_pull(raw, wk[...], cos_k[ch], sin_k[ch], total[0] * SM_SCALE)
-            dk_out[head, ch] = grad_raw.astype(jnp.bfloat16)
-            dv_out[head, ch] = total[1].astype(jnp.bfloat16)
+            dkv_out[head, 0, ch] = grad_raw.astype(jnp.bfloat16)
+            dkv_out[head, 1, ch] = total[1].astype(jnp.bfloat16)
             dw_acc[1] += terms
+        out_copy(head).start()
 
     def home_head(h):
         for ch in range(2):
@@ -291,9 +309,9 @@
 
         @pl.loop(0, num_chips)
         def _(j):
-            first_order = jnp.where(j == 0, 0, jnp.where(j == 1, 1, jnp.where(j == 2, 3, 2)))
-            last_order = jnp.where(j == 0, 2, jnp.where(j == 1, 1, jnp.where(j == 2, 3, 0)))
-            off = jnp.where(last, last_order, first_order)
+            orders = [sum(off * 4 ** i for i, off in enumerate(order)) for order in ((0, 3, 1, 2), (0, 1, 3, 2), (3, 1, 0, 2), (2, 1, 3, 0))]
+            order = jnp.where(h == 0, orders[0], jnp.where(last, orders[3], jnp.where(h == 1, orders[1], orders[2])))
+            off = order // jnp.where(j == 0, 1, jnp.where(j == 1, 4, jnp.where(j == 2, 16, 64))) % 4
 
             @pl.when(off == 2)
             def _():
@@ -348,23 +366,23 @@
                 nb_wait(of_head, 1)
                 relay_each(of_head, lambda copy: copy.start())
 
-                @pl.when(of_head + 2 < heads)
-                def _():
-                    nb_each(of_head + 2, lambda copy: copy.start())
-
             @pl.when((h == 0) & (j == 0))
             def _():
                 pass_keys(0)
 
-            @pl.when((j == 3) & (h + 1 < heads))
+            @pl.when((h + 1 < heads) & (j == jnp.where(h == 0, 2, 0)))
             def _():
                 pass_keys(h + 1)
 
-            @pl.when((j == 0) & (h > 0))
+            @pl.when((h + 2 < heads) & (j == jnp.where(h == 0, 1, 0)))
+            def _():
+                nb_each(h + 2, lambda copy: copy.start())
+
+            @pl.when((h > 0) & (j == jnp.where(last, 0, 2)))
             def _():
                 forward_each(h - 1, start_forward)
 
-            @pl.when((j == 2) & last)
+            @pl.when(last & (j == 1))
             def _():
                 forward_each(h, start_forward)
 
@@ -392,6 +410,7 @@
     pl.semaphore_wait(barrier, num_chips * CORES - 1)
 
     nb_each(0, lambda copy: copy.start())
+    in_copy(0).start()
 
     @pl.loop(0, heads)
     def _(h):
@@ -403,19 +422,24 @@
             local.start()
 
     nb_each(1, lambda copy: copy.start())
-
+    in_copy(1).start()
+    in_copy(2).start()
+    wq[...] = jnp.broadcast_to(wq_row[...], (chunk_len, HEAD_DIM)).T
+    in_copy(0).wait()
+    in_copy(1).wait()
+    in_copy(2).wait()
     dw_acc[...] = jnp.zeros_like(dw_acc)
     dwq_acc[...] = jnp.zeros_like(dwq_acc)
 
-    @pl.loop(0, heads + 2)
+    @pl.loop(0, heads + 3)
     def _(h):
         @pl.when(h < heads)
         def _():
             compute_head(h)
 
-        @pl.when(h >= 2)
+        @pl.when(h >= 3)
         def _():
-            home_head(h - 2)
+            home_head(h - 3)
 
     dw_acc[0] = dwq_acc[...].T.reshape(-1, 8, HEAD_DIM).sum(0)
     for step in range(1, num_chips * CORES):
@@ -446,6 +470,8 @@
             out.wait_send()
             arriving.wait_recv()
             local.wait()
+        out_copy(h).wait()
+        out_copy(heads + h).wait()
 
     for step in range(1, num_chips * CORES):
         peer = (me + step) % (num_chips * CORES)
@@ -454,7 +480,7 @@
     dw_out[...] = dw_all[...].sum(0).sum(1)
 
 
-def prepare_kernel(q_ref, do_ref, out_ref, k_ref, v_ref, lse_ref, cos_k, sin_k, wk, q_out, do_out, st_out, kv_out, k_out):
+def prepare_kernel(q_ref, do_ref, out_ref, k_ref, v_ref, lse_ref, k_table, wk, q_out, do_out, st_out, kv_out, k_out):
     rows, num_heads = q_ref.shape[0], q_ref.shape[1]
     kv_heads = k_ref.shape[1]
     f32, bf16 = jnp.float32, jnp.bfloat16
@@ -466,17 +492,17 @@
     q_out[:, 0] = by_head(q_ref[...].astype(f32)).astype(bf16).reshape(kv_heads, -1, rows, HEAD_DIM)
     do_out[:, 0] = by_head(d_out).astype(bf16).reshape(kv_heads, -1, rows, HEAD_DIM)
     delta = jnp.sum(d_out * out_ref[...].astype(f32), axis=-1)
-    st_out[:, 0, 0] = (lse_ref[...] * LOG2E).T.reshape(kv_heads, -1, rows)
+    st_out[:, 0, 0] = (lse_ref[...] * LOG2E).reshape(kv_heads, -1, rows)
     st_out[:, 0, 1] = delta.T.reshape(kv_heads, -1, rows)
     raw = k_ref[...].astype(f32)
     normed = raw * inverse_rms(raw) * wk[...]
-    key = normed * cos_k[0][:, None] + swap_halves(normed) * sin_k[0][:, None]
+    key = normed * k_table[0, 0][:, None] + swap_halves(normed) * k_table[1, 0][:, None]
     kv_out[:, 0, 0] = by_head(key).astype(bf16)
     kv_out[:, 0, 1] = by_head(v_ref[...].astype(f32)).astype(bf16)
     k_out[:, 0] = by_head(raw).astype(bf16)
 
 
-def prepare(q_raw, d_out, out_fwd, k_raw, v_proj, lse_fwd, cos_k, sin_k, wk, rows=128):
+def prepare(q_raw, d_out, out_fwd, k_raw, v_proj, lse_t, k_tables, wk, rows=128):
     local_rows, num_heads, _ = q_raw.shape
     kv_heads = k_raw.shape[1]
     per_kv, chunk_len = num_heads // kv_heads, local_rows // 2
@@ -484,12 +510,12 @@
     bf16 = jnp.bfloat16
     rows_q = pl.BlockSpec((rows, num_heads, HEAD_DIM), lambda i: (i, 0, 0))
     rows_k = pl.BlockSpec((rows, kv_heads, HEAD_DIM), lambda i: (i, 0, 0))
-    table = pl.BlockSpec((1, rows, HEAD_DIM), lambda i: (i // parts, i % parts, 0))
+    table = pl.BlockSpec((2, 1, rows, HEAD_DIM), lambda i: (0, i // parts, i % parts, 0))
     heads_q = pl.BlockSpec((kv_heads, 1, per_kv, rows, HEAD_DIM), lambda i: (0, i // parts, 0, i % parts, 0))
     return pl.pallas_call(
         prepare_kernel,
         grid=(2 * parts,),
-        in_specs=[rows_q, rows_q, rows_q, rows_k, rows_k, pl.BlockSpec((rows, num_heads), lambda i: (i, 0)), table, table,
+        in_specs=[rows_q, rows_q, rows_q, rows_k, rows_k, pl.BlockSpec((num_heads, rows), lambda i: (0, i)), table,
                   pl.BlockSpec((1, HEAD_DIM), lambda i: (0, 0))],
         out_specs=[heads_q, heads_q,
                    pl.BlockSpec((kv_heads, 1, 2, per_kv, rows), lambda i: (0, i // parts, 0, 0, i % parts)),
@@ -502,34 +528,34 @@
                    jax.ShapeDtypeStruct((kv_heads, 2, chunk_len, HEAD_DIM), bf16)],
         compiler_params=pltpu.CompilerParams(vmem_limit_bytes=48 * 2 ** 20),
         name='prepare',
-    )(q_raw, d_out, out_fwd, k_raw, v_proj, lse_fwd, cos_k, sin_k, wk)
-
-
-def finish_kernel(dq_ref, dk_ref, dv_ref, dq_out, dk_out, dv_out):
-    for src, dst in ((dq_ref, dq_out), (dk_ref, dk_out), (dv_ref, dv_out)):
+    )(q_raw, d_out, out_fwd, k_raw, v_proj, lse_t, k_tables, wk)
+
+
+def finish_kernel(dq_ref, dkv_ref, dq_out, dk_out, dv_out):
+    for src, dst in ((dq_ref, dq_out), (dkv_ref.at[:, 0], dk_out), (dkv_ref.at[:, 1], dv_out)):
         by_head = src[:, 0].reshape(-1, src.shape[-2], HEAD_DIM).astype(jnp.float32)
         dst[...] = jnp.swapaxes(by_head, 0, 1).astype(jnp.bfloat16)
 
 
-def finish(dq, dk, dv, rows=128):
+def finish(dq, dkv, rows=128):
     kv_heads, _, per_kv, chunk_len, _ = dq.shape
     parts = chunk_len // rows
     num_heads = kv_heads * per_kv
-    heads_k = pl.BlockSpec((kv_heads, 1, rows, HEAD_DIM), lambda i: (0, i // parts, i % parts, 0))
+    heads_k = pl.BlockSpec((kv_heads, 2, 1, rows, HEAD_DIM), lambda i: (0, 0, i // parts, i % parts, 0))
     rows_k = pl.BlockSpec((rows, kv_heads, HEAD_DIM), lambda i: (i, 0, 0))
     out_k = jax.ShapeDtypeStruct((2 * chunk_len, kv_heads, HEAD_DIM), jnp.bfloat16)
     return pl.pallas_call(
         finish_kernel,
         grid=(2 * parts,),
-        in_specs=[pl.BlockSpec((kv_heads, 1, per_kv, rows, HEAD_DIM), lambda i: (0, i // parts, 0, i % parts, 0)), heads_k, heads_k],
+        in_specs=[pl.BlockSpec((kv_heads, 1, per_kv, rows, HEAD_DIM), lambda i: (0, i // parts, 0, i % parts, 0)), heads_k],
         out_specs=[pl.BlockSpec((rows, num_heads, HEAD_DIM), lambda i: (i, 0, 0)), rows_k, rows_k],
         out_shape=[jax.ShapeDtypeStruct((2 * chunk_len, num_heads, HEAD_DIM), jnp.bfloat16), out_k, out_k],
         compiler_params=pltpu.CompilerParams(vmem_limit_bytes=48 * 2 ** 20),
         name='finish',
-    )(dq, dk, dv)
-
-
-def attn_grads(num_chips, q, d_out, stats, kv, k_raw, cos_q, sin_q, cos_k, sin_k, wq, wk):
+    )(dq, dkv)
+
+
+def attn_grads(num_chips, q, d_out, stats, kv, k_raw, tables, k_tables, wq, wk):
     kv_heads, _, rows, _ = q.shape
     chunk_len = kv.shape[3]
     heads = kv_heads // CORES
@@ -539,11 +565,16 @@
     any_spec, vmem = pl.BlockSpec(memory_space=pl.ANY), pl.BlockSpec(memory_space=pltpu.VMEM)
     return pl.pallas_call(
         functools.partial(attn_kernel, num_chips),
-        in_specs=[any_spec] * 4 + [vmem] * 7,
-        out_specs=[any_spec, vmem, vmem, vmem],
-        out_shape=[jax.ShapeDtypeStruct(q.shape, bf16), jax.ShapeDtypeStruct(k_raw.shape, bf16),
-                   jax.ShapeDtypeStruct(k_raw.shape, bf16), jax.ShapeDtypeStruct((2, HEAD_DIM), f32)],
+        in_specs=[any_spec] * 7 + [vmem] * 2,
+        out_specs=[any_spec, any_spec, vmem],
+        out_shape=[jax.ShapeDtypeStruct(q.shape, bf16), jax.ShapeDtypeStruct((kv_heads, 2) + k_raw.shape[1:], bf16),
+                   jax.ShapeDtypeStruct((2, HEAD_DIM), f32)],
         scratch_shapes=[
+            pltpu.VMEM(k_raw.shape, bf16),
+            pltpu.VMEM(tables.shape, f32),
+            pltpu.VMEM(k_tables.shape, f32),
+            pltpu.VMEM((HEAD_DIM, chunk_len), f32),
+            pltpu.VMEM((kv_heads, 2) + k_raw.shape[1:], bf16),
             pltpu.VMEM((heads, 4, rows, HEAD_DIM), bf16),
             pltpu.VMEM((heads, 4, rows, HEAD_DIM), bf16),
             pltpu.VMEM((heads, 4) + stats.shape[2:], f32),
@@ -554,8 +585,8 @@
             pltpu.VMEM((4, HEAD_DIM, rows), bf16),
             pltpu.VMEM((4, HEAD_DIM, rows), f32),
             pltpu.VMEM((HEAD_DIM, chunk_len), bf16),
-            pltpu.VMEM((chunk_len, rows), bf16),
-            pltpu.VMEM((chunk_len, rows), bf16),
+            pltpu.VMEM((2, chunk_len, rows), bf16),
+            pltpu.VMEM((2, chunk_len, rows), bf16),
             pltpu.VMEM((4,) + half, f32),
             pltpu.VMEM((heads, 4) + half, f32),
             pltpu.VMEM((heads, 2) + half, f32),
@@ -576,11 +607,12 @@
             sem((heads, 2)), sem((heads, 2)),
             sem((heads, 2)), sem((heads, 2)), sem((heads, 2)),
             sem((num_chips * CORES,)), sem((num_chips * CORES,)),
+            sem((3,)), sem((kv_heads,)),
         ],
         compiler_params=pltpu.CompilerParams(vmem_limit_bytes=60 * 2 ** 20, collective_id=0, has_side_effects=True),
         cost_estimate=pl.CostEstimate(flops=50_000_000_000, bytes_accessed=64_000_000, transcendentals=40_000_000),
         name='attn_grads',
-    )(q, d_out, stats, kv, k_raw, cos_q, sin_q, cos_k, sin_k, wq, wk)
+    )(q, d_out, stats, kv, k_raw, tables, k_tables, wq, wk)
 
 
 def solution(mesh):
@@ -598,17 +630,18 @@
         num_chunks = 2 * cp_size
         offsets = jnp.arange(chunk_len)
         chip_chunks = jnp.stack([2 * chip, 2 * chip + 1, num_chunks - 2 - 2 * chip, num_chunks - 1 - 2 * chip])
-        cos_q, sin_q = rope_tables(chip_chunks[:, None] * chunk_len + offsets)
+        inv_freq = ROPE_THETA ** (-jnp.arange(0, HEAD_DIM, 2).astype(jnp.float32) / HEAD_DIM)
+        angles = inv_freq[None, :, None] * (chip_chunks[:, None] * chunk_len + offsets).astype(jnp.float32)[:, None, :]
+        cos_t, sin_t = jnp.cos(angles), jnp.sin(angles)
+        tables = jnp.stack([jnp.concatenate([cos_t, cos_t], axis=1), jnp.concatenate([-sin_t, sin_t], axis=1)])
         dev_chunks = jnp.stack([dev_rank, num_chunks - 1 - dev_rank])
-        cos_k, sin_k = rope_tables(dev_chunks[:, None] * chunk_len + offsets)
-
-        q_h, do_h, stats, kv, k_h = prepare(q_raw, d_out, out_fwd, k_raw, v_proj, lse_fwd, cos_k, sin_k, k_norm[None])
+        k_tables = jnp.stack(rope_tables(dev_chunks[:, None] * chunk_len + offsets))
+
+        q_h, do_h, stats, kv, k_h = prepare(q_raw, d_out, out_fwd, k_raw, v_proj, lse_fwd.T, k_tables, k_norm[None])
         stacked = (kv_heads, 2, per_kv * chunk_len, HEAD_DIM)
-        cos_qt, sin_qt = jnp.swapaxes(cos_q, 1, 2), jnp.swapaxes(sin_q, 1, 2)
-        wq_t = jnp.broadcast_to(q_norm[:, None], (HEAD_DIM, chunk_len))
-        dq, dk, dv, weights = attn_grads(num_chips, q_h.reshape(stacked), do_h.reshape(stacked), stats, kv, k_h,
-                                         cos_qt, sin_qt, cos_k, sin_k, wq_t, k_norm[None])
-        dq_raw, dk_raw, dv_home = finish(dq.reshape(q_h.shape), dk, dv)
+        dq, dkv, weights = attn_grads(num_chips, q_h.reshape(stacked), do_h.reshape(stacked), stats, kv, k_h,
+                                      tables, k_tables, q_norm[None], k_norm[None])
+        dq_raw, dk_raw, dv_home = finish(dq.reshape(q_h.shape), dkv)
         return dq_raw, dk_raw, dv_home, weights[0], weights[1]
 
     row_spec = P(('dp', 'cp'))

time: 200 us -> 180 us (0.900)
  Pallas kernels: 187 us -> 170 us
  local copies, waits for them, and re-layouts: 8.51 us -> 5.13 us
    pallas_call x1, Pallas kernels: 168 us -> 152 us  [attn_grads(): pl.pallas_call(functools.partial(attn_kernel, num_chips), in_specs=[any_s...]
    unnamed x23 -> x20, local copies, waits for them, and re-layouts: 6.42 us -> 4.61 us
where the time goes in v4:
time: 180 us
  Pallas kernels  170 us (94%)
  local copies, waits for them, and re-layouts  5.13 us (3%)
  other arithmetic  3.71 us (2%)
    pallas_call x1, Pallas kernels, attn_grads(): pl.pallas_call(functools.partial(attn_kernel, num_chips), in_specs=[any_s...  152 us
    pallas_call x1, Pallas kernels, prepare(): pl.pallas_call(prepare_kernel, grid=(2 * parts,), in_specs=[rows_q, rows_...  12.2 us
    pallas_call x1, Pallas kernels, finish(): pl.pallas_call(finish_kernel, grid=(2 * parts,), in_specs=[pl.BlockSpec((...  6.26 us
    unnamed x20, local copies, waits for them, and re-layouts  4.61 us

profile of v4, /device:TPU:81, one launch (start us, length us, event | category | flops | bytes accessed | tf_op | source)
XLA Modules:
  0.0 179.7 jit_solution(10907360276243794800)
XLA Ops:
  0.6 0.0 copy-start.5
  0.6 0.0 copy-start.4
  0.7 0.0 copy-start.3
  0.7 0.0 copy-start.2
  0.7 0.1 add_multiply_fusion.1
  0.8 0.1 add_multiply_fusion
  0.9 0.1 add_convert_fusion.1
  0.9 0.1 add_convert_fusion
  1.0 1.0 multiply_cosine_fusion
  2.0 0.1 maximum_bitcast_fusion
  2.1 1.1 pad_maximum_fusion.tables_hbm
  3.2 1.0 multiply_cosine_fusion.1
  4.2 0.2 maximum_bitcast_fusion.2
  4.4 0.0 copy-done.5
  4.4 0.0 copy-done.4
  4.5 0.0 copy-done.3
  4.5 0.0 copy-done.2
  4.5 0.0 copy-start.1
  4.5 12.2 %prepare.1 = (bf16[8,2,4,256,128]{4,3,2,1,0:T(8,128)(2,1)}, bf16[8,2,4,256,128]{4,3,2,1,0:T(8,128)(2,1)}, f32[8,2,2,4,256]{4,3,2,1,0:T(4,128)S(1)}, bf16[8,2,2,2...) custom-call(bf16[512,32,128]{2,1,0:T(8,128)(2,1)} %q_ref.1, bf16[512,32,128]{2,1,0:T(8,128)(2,1)} %do_ref.1, ...), custom_call_target="tpu_custom_call" | custom-call | tf_op jit(solution)/shard_map/prepare/pallas_call | solution.py:515
  16.7 0.0 copy-done.1
  16.7 0.0 copy-start.6
  16.7 1.4 copy-done.6
  18.1 0.0 copy-start.7
  18.1 1.0 copy-done.7
  19.1 0.7 copy-done.8
  19.7 151.6 %attn_grads.1 = (bf16[8,2,1024,128]{3,2,1,0:T(8,128)(2,1)}, bf16[8,2,2,256,128]{4,3,2,1,0:T(8,128)(2,1)}, f32[2,128]{1,0:T(2,128)}) custom-call(bf16[8,2,1024,128]{3,2,1,0:T(8,128)(2,1)} %bitcast.28, bf16[8,2,1024,128]{3,2,1,0:T(8,128)(2,1)} %bitcast.29, f32[8,2,2,4,256]{4,3,2,1,0:T(4,128)} %copy-done.8, bf16[8,2,2,256,128]{4,3,2,1,0:T(8,128)(2,1)} %copy-done.6, ...), custom_call_target="tpu_custom_call" | custom-call | flops 49999998976 | bytes 64000000 | tf_op jit(solution)/shard_map/attn_grads/pallas_call | solution.py:566
  171.3 0.0 copy-start.9
  171.3 0.0 copy-start
  171.3 1.6 copy-done
  172.9 6.3 %finish.1 = (bf16[512,32,128]{2,1,0:T(8,128)(2,1)}, bf16[512,8,128]{2,1,0:T(8,128)(2,1)}, bf16[512,8,128]{2,1,0:T(8,128)(2,1)}) custom-call(bf16[8,2,4,256,128]{4,3,2,1,0:T(8,128)(2,1)} %bitcast.27, bf16[8,2,2,256,128]{4,3,2,1,0:T(8,128)(2,1)S(1)} %copy-done), custom_call_target="tpu_custom_call" | custom-call | tf_op jit(solution)/shard_map/finish/pallas_call | solution.py:547
  179.1 0.0 copy-done.9
  179.1 0.5 slice_bitcast_fusion
  (3 shorter events, 0.0 us)
Async XLA Ops:
  0.6 3.8 %copy-start.5 = (f32[128]{0:T(128)S(1)}, f32[128]{0:T(128)}, u32[]{:S(2)}) copy-start(f32[128]{0:T(128)} %param.15) | copy-start | bytes 1540
  0.6 3.8 %copy-start.4 = (f32[512,32]{0,1:T(8,128)S(1)}, f32[512,32]{0,1:T(8,128)}, u32[]{:S(2)}) copy-start(f32[512,32]{0,1:T(8,128)} %param.12) | copy-start | bytes 196612
  0.7 3.8 %copy-start.3 = (bf16[512,8,128]{2,1,0:T(8,128)(2,1)S(1)}, bf16[512,8,128]{2,1,0:T(8,128)(2,1)}, u32[]{:S(2)}) copy-start(bf16[512,8,128]{2,1,0:T(8,128)(2,1)} %v_ref.1) | copy-start | bytes 3145732
  0.7 3.8 %copy-start.2 = (bf16[512,8,128]{2,1,0:T(8,128)(2,1)S(1)}, bf16[512,8,128]{2,1,0:T(8,128)(2,1)}, u32[]{:S(2)}) copy-start(bf16[512,8,128]{2,1,0:T(8,128)(2,1)} %k_ref.1) | copy-start | bytes 3145732
  4.5 12.2 %copy-start.1 = (f32[2,2,256,128]{3,2,1,0:T(8,128)}, f32[2,2,256,128]{3,2,1,0:T(8,128)S(1)}, u32[]{:S(2)}) copy-start(f32[2,2,256,128]{3,2,1,0:T(8,128)S(1)} %pad_maximum_fusion.1.k_table.k_tables_hbm) | copy-start | bytes 1572868
  16.7 1.4 copy-start.6
  18.1 1.0 copy-start.7
  19.0 0.7 copy-start.8
  171.3 7.9 %copy-start.9 = (f32[2,128]{1,0:T(2,128)S(1)}, f32[2,128]{1,0:T(2,128)}, u32[]{:S(2)}) copy-start(f32[2,128]{1,0:T(2,128)} %get-tuple-element.26) | copy-start | bytes 3076
  171.3 1.6 copy-start

commit v5 on v4

--- a/solution.py
+++ b/solution.py
@@ -426,8 +426,6 @@
     in_copy(2).start()
     wq[...] = jnp.broadcast_to(wq_row[...], (chunk_len, HEAD_DIM)).T
     in_copy(0).wait()
-    in_copy(1).wait()
-    in_copy(2).wait()
     dw_acc[...] = jnp.zeros_like(dw_acc)
     dwq_acc[...] = jnp.zeros_like(dwq_acc)
 
@@ -436,6 +434,11 @@
         @pl.when(h < heads)
         def _():
             compute_head(h)
+
+        @pl.when(h == 3)
+        def _():
+            in_copy(1).wait()
+            in_copy(2).wait()
 
         @pl.when(h >= 3)
         def _():
@@ -526,7 +529,7 @@
                    jax.ShapeDtypeStruct((kv_heads, 2, 2, per_kv, chunk_len), jnp.float32),
                    jax.ShapeDtypeStruct((kv_heads, 2, 2, chunk_len, HEAD_DIM), bf16),
                    jax.ShapeDtypeStruct((kv_heads, 2, chunk_len, HEAD_DIM), bf16)],
-        compiler_params=pltpu.CompilerParams(vmem_limit_bytes=48 * 2 ** 20),
+        compiler_params=pltpu.CompilerParams(vmem_limit_bytes=63 * 2 ** 20),
         name='prepare',
     )(q_raw, d_out, out_fwd, k_raw, v_proj, lse_t, k_tables, wk)
 
@@ -537,7 +540,7 @@
         dst[...] = jnp.swapaxes(by_head, 0, 1).astype(jnp.bfloat16)
 
 
-def finish(dq, dkv, rows=128):
+def finish(dq, dkv, rows=64):
     kv_heads, _, per_kv, chunk_len, _ = dq.shape
     parts = chunk_len // rows
     num_heads = kv_heads * per_kv
@@ -550,7 +553,7 @@
         in_specs=[pl.BlockSpec((kv_heads, 1, per_kv, rows, HEAD_DIM), lambda i: (0, i // parts, 0, i % parts, 0)), heads_k],
         out_specs=[pl.BlockSpec((rows, num_heads, HEAD_DIM), lambda i: (i, 0, 0)), rows_k, rows_k],
         out_shape=[jax.ShapeDtypeStruct((2 * chunk_len, num_heads, HEAD_DIM), jnp.bfloat16), out_k, out_k],
-        compiler_params=pltpu.CompilerParams(vmem_limit_bytes=48 * 2 ** 20),
+        compiler_params=pltpu.CompilerParams(vmem_limit_bytes=63 * 2 ** 20),
         name='finish',
     )(dq, dkv)
 
@@ -609,7 +612,7 @@
             sem((num_chips * CORES,)), sem((num_chips * CORES,)),
             sem((3,)), sem((kv_heads,)),
         ],
-        compiler_params=pltpu.CompilerParams(vmem_limit_bytes=60 * 2 ** 20, collective_id=0, has_side_effects=True),
+        compiler_params=pltpu.CompilerParams(vmem_limit_bytes=63 * 2 ** 20, collective_id=0, has_side_effects=True),
         cost_estimate=pl.CostEstimate(flops=50_000_000_000, bytes_accessed=64_000_000, transcendentals=40_000_000),
         name='attn_grads',
     )(q, d_out, stats, kv, k_raw, tables, k_tables, wq, wk)

time: 180 us -> 179 us (level)
  local copies, waits for them, and re-layouts: 5.13 us -> 0.52 us
  Pallas kernels: 170 us -> 173 us
    unnamed x20 -> x2, local copies, waits for them, and re-layouts: 4.61 us -> 0.01 us
    pallas_call x1, Pallas kernels: 6.26 us -> 8.55 us  [finish(): pl.pallas_call(finish_kernel, grid=(2 * parts,), in_specs=[pl.BlockSpec((...]
where the time goes in v5:
time: 179 us
  Pallas kernels  173 us (97%)
  other arithmetic  4.53 us (3%)
    pallas_call x1, Pallas kernels, attn_grads(): pl.pallas_call(functools.partial(attn_kernel, num_chips), in_specs=[any_s...  152 us
    pallas_call x1, Pallas kernels, prepare(): pl.pallas_call(prepare_kernel, grid=(2 * parts,), in_specs=[rows_q, rows_...  13.1 us
    pallas_call x1, Pallas kernels, finish(): pl.pallas_call(finish_kernel, grid=(2 * parts,), in_specs=[pl.BlockSpec((...  8.55 us

profile of v5, /device:TPU:81, one launch (start us, length us, event | category | flops | bytes accessed | tf_op | source)
XLA Modules:
  0.0 179.0 jit_solution(13946526102213088231)
XLA Ops:
  0.6 0.1 add_multiply_fusion.1
  0.7 0.1 add_multiply_fusion
  0.8 0.1 add_convert_fusion.1
  0.9 0.1 add_convert_fusion
  1.0 1.0 multiply_cosine_fusion
  2.0 0.1 maximum_bitcast_fusion
  2.1 1.1 pad_maximum_fusion.tables_hbm
  3.1 1.0 multiply_cosine_fusion.1
  4.1 0.2 maximum_bitcast_fusion.2
  4.3 0.9 pad_maximum_fusion.1.k_table.k_tables_hbm
  5.2 13.1 %prepare.1 = (bf16[8,2,4,256,128]{4,3,2,1,0:T(8,128)(2,1)}, bf16[8,2,4,256,128]{4,3,2,1,0:T(8,128)(2,1)}, f32[8,2,2,4,256]{4,3,2,1,0:T(4,128)}, bf16[8,2,2,256,1...) custom-call(bf16[512,32,128]{2,1,0:T(8,128)(2,1)} %q_ref.1, bf16[512,32,128]{2,1,0:T(8,128)(2,1)} %do_ref.1, ...), custom_call_target="tpu_custom_call" | custom-call | tf_op jit(solution)/shard_map/prepare/pallas_call | solution.py:518
  18.3 151.6 %attn_grads.1 = (bf16[8,2,1024,128]{3,2,1,0:T(8,128)(2,1)}, bf16[8,2,2,256,128]{4,3,2,1,0:T(8,128)(2,1)}, f32[2,128]{1,0:T(2,128)}) custom-call(bf16[8,2,1024,128]{3,2,1,0:T(8,128)(2,1)} %bitcast.28, bf16[8,2,1024,128]{3,2,1,0:T(8,128)(2,1)} %bitcast.29, f32[8,2,2,4,256]{4,3,2,1,0:T(4,128)} %get-tuple-element.18.st_hbm, ...), custom_call_target="tpu_custom_call" | custom-call | flops 49999998976 | bytes 64000000 | tf_op jit(solution)/shard_map/attn_grads/pallas_call | solution.py:569
  169.9 0.0 copy-start
  169.9 8.6 %finish.1 = (bf16[512,32,128]{2,1,0:T(8,128)(2,1)}, bf16[512,8,128]{2,1,0:T(8,128)(2,1)}, bf16[512,8,128]{2,1,0:T(8,128)(2,1)}) custom-call(bf16[8,2,4,256,128]{4,3,2,1,0:T(8,128)(2,1)} %bitcast.24, bf16[8,2,2,256,128]{4,3,2,1,0:T(8,128)(2,1)} %get-tuple-element.22.dkv_ref), custom_call_target="tpu_custom_call" | custom-call | tf_op jit(solution)/shard_map/finish/pallas_call | solution.py:550
  178.5 0.0 copy-done
  178.5 0.5 slice_bitcast_fusion
  (1 shorter events, 0.0 us)
Async XLA Ops:
  169.9 8.6 %copy-start = (f32[2,128]{1,0:T(2,128)S(1)}, f32[2,128]{1,0:T(2,128)}, u32[]{:S(2)}) copy-start(f32[2,128]{1,0:T(2,128)} %get-tuple-element.26) | copy-start | bytes 3076
